TPU v7x, 128 devices: a whole 4x4x4 slice. The times are simulated.
128 devices in a mesh: lat: 16 (over y_hi, x, core), lon: 8 (over z, y_lo).
Axes of the slice: x: 4, y: 4 (y_hi: 2, y_lo: 2; y = y_hi * 2 + y_lo), z: 4, core: 2. Of those that a mesh axis runs over, the one named last changes fastest.
Arguments:
- ocean_state: bfloat16 [144, 2048, 128], P('lat', 'lon'), may hold values from -6 to 6
- cotangent: bfloat16 [144, 2048, 128], P('lat', 'lon'), may hold values from -6 to 6
- atm_embed: bfloat16 [65536, 256], P(('lat', 'lon')), may hold values from -6 to 6
- projection: bfloat16 [256, 128], replicated, may hold values from -0.375 to 0.375
- dw_kernel: float32 [7, 7, 128], replicated, may hold values from -0.875 to 0.875
- norm_gain: float32 [128], replicated, may hold values from 0.25 to 1.75
- w_in: bfloat16 [128, 512], replicated, may hold values from -0.5 to 0.5
- w_out: bfloat16 [512, 128], replicated, may hold values from -0.25 to 0.25
- margin_index: int32 [4, 144, 2048], P(None, 'lat', 'lon'), may hold values from 0 to 1023
- margin_weight: float32 [4, 144, 2048], P(None, 'lat', 'lon'), may hold values from 0.05 to 0.6
- sea_mask: int32 [144, 2048], P('lat', 'lon'), may hold values 0 or 1
Outputs:
- grad_state: float32 [144, 2048, 128], P('lat', 'lon')
- grad_embed: float32 [65536, 256], P(('lat', 'lon'))
- grad_projection: float32 [256, 128], replicated
- grad_kernel: float32 [7, 7, 128], replicated
- grad_gain: float32 [128], replicated
- grad_w_in: float32 [128, 512], replicated
- grad_w_out: float32 [512, 128], replicated
All inputs are finite; a program needn't handle non-finite values. No bound on the sum of `sea_mask` on one device may be relied on, other than what follows from the above.
Results may differ from a plain program's by a relative error of at most 0.0058.
Values may be sent and summed in bfloat16 or wider, within the bound.
A program may use at most 64 MiB of HBM per device.

v0:
```python
import jax
import jax.numpy as jnp
from jax import lax
from jax.sharding import PartitionSpec as P

EPSILON = 1e-05


def shifted(x, axis, by):
    size = lax.axis_size(axis)
    pairs = [(i, i + by) for i in range(size) if 0 <= i + by < size]
    return lax.ppermute(x, axis, pairs)


def with_halo(block, sides, width):
    for axis, dim in sides:
        count = lax.axis_size(axis)
        forward = [(i, i + 1) for i in range(count - 1)]
        forward.append((count - 1, 0))
        backward = [(target, source) for source, target in forward]
        low = lax.ppermute(
            lax.slice_in_dim(block, block.shape[dim] - width, None, axis=dim), axis, forward
        )
        high = lax.ppermute(lax.slice_in_dim(block, 0, width, axis=dim), axis, backward)
        block = jnp.concatenate([low, block, high], axis=dim)
    return block


def depthwise(padded, kernel):
    height = padded.shape[0] - 6
    width = padded.shape[1] - 6
    total = jnp.zeros((height, width, padded.shape[2]), jnp.float32)
    for row_tap in range(7):
        for col_tap in range(7):
            total = (
                total
                + padded[row_tap : row_tap + height, col_tap : col_tap + width]
                * kernel[row_tap, col_tap]
            )
    return total


def depthwise_back(padded, kernel):
    height = padded.shape[0] - 6
    width = padded.shape[1] - 6
    total = jnp.zeros((height, width, padded.shape[2]), jnp.float32)
    for row_tap in range(7):
        for col_tap in range(7):
            total = (
                total
                + padded[6 - row_tap : 6 - row_tap + height, 6 - col_tap : 6 - col_tap + width]
                * kernel[row_tap, col_tap]
            )
    return total


def kernel_grad(grad, padded):
    height = grad.shape[0]
    width = grad.shape[1]
    pieces = []
    for row_tap in range(7):
        for col_tap in range(7):
            pieces.append(
                jnp.sum(
                    grad * padded[row_tap : row_tap + height, col_tap : col_tap + width],
                    axis=(0, 1),
                )
            )
    return jnp.stack(pieces).reshape(7, 7, grad.shape[2])


def norm_forward(field):
    center = field - jnp.mean(field, axis=-1, keepdims=True)
    sigma = jnp.sqrt(jnp.mean(center * center, axis=-1, keepdims=True) + EPSILON)
    return (center / sigma, sigma)


def norm_back(g_ln, normed, sigma, gain):
    gain_grad = jnp.sum(g_ln * normed, axis=(0, 1))
    g_norm = g_ln * gain
    g_field = (
        g_norm
        - jnp.mean(g_norm, axis=-1, keepdims=True)
        - normed * jnp.mean(g_norm * normed, axis=-1, keepdims=True)
    ) / sigma
    return (g_field, gain_grad)


def gelu_tanh(value):
    return jax.nn.gelu(value, approximate=True)


def mlp_back(ln_rows, gy_rows, w_in, w_out):
    pre_act = jnp.dot(ln_rows, w_in, preferred_element_type=jnp.float32)
    hidden, pullback = jax.vjp(gelu_tanh, pre_act)
    hidden = hidden.astype(jnp.bfloat16)
    grad_out = lax.dot_general(
        hidden, gy_rows, (((0,), (0,)), ((), ())), preferred_element_type=jnp.float32
    )
    g_hidden = lax.dot_general(
        gy_rows, w_out, (((1,), (1,)), ((), ())), preferred_element_type=jnp.float32
    )
    g_pre = pullback(g_hidden)[0].astype(jnp.bfloat16)
    grad_in = lax.dot_general(
        ln_rows, g_pre, (((0,), (0,)), ((), ())), preferred_element_type=jnp.float32
    )
    g_ln = lax.dot_general(
        g_pre, w_in, (((1,), (1,)), ((), ())), preferred_element_type=jnp.float32
    )
    return (g_ln, grad_in, grad_out)


def clear_ends(padded):
    band = lax.axis_index("lat")
    bands = lax.axis_size("lat")
    position = jnp.arange(padded.shape[0], dtype=jnp.int32)
    dropped = (band == 0) & (position < 3) | (band == bands - 1) & (position >= padded.shape[0] - 3)
    return padded * jnp.where(dropped, 0.0, 1.0).astype(jnp.float32)[:, None, None]


def margin_block(index_rows, weight_rows, slots):
    columns = jnp.arange(slots, dtype=jnp.int32)[None, :]
    dense = jnp.zeros((index_rows.shape[1], slots), jnp.float32)
    for slot in range(index_rows.shape[0]):
        dense = dense + jnp.where(
            index_rows[slot][:, None] == columns, weight_rows[slot][:, None], 0.0
        )
    return dense


def block_rows(height, width):
    limit = max(1, 2048 // width)
    best = 1
    for count in range(1, height + 1):
        if height % count == 0 and count <= limit:
            best = count
    return best


def shards(
    ocean_state,
    cotangent,
    atm_embed,
    projection,
    dw_kernel,
    norm_gain,
    w_in,
    w_out,
    margin_index,
    margin_weight,
    sea_mask,
):
    cells_atm = atm_embed.shape[0]
    channels = projection.shape[1]
    height = ocean_state.shape[0]
    width = ocean_state.shape[1]
    margins = margin_index.shape[0]
    slots = 2 * cells_atm
    group = block_rows(height, width) * width
    blocks = height * width // group
    index_blocks = jnp.transpose(margin_index.reshape(margins, blocks, group), (1, 0, 2))
    weight_blocks = jnp.transpose(margin_weight.reshape(margins, blocks, group), (1, 0, 2))
    next_embed = shifted(atm_embed, "lat", -1)
    window_embed = jnp.concatenate([atm_embed, next_embed], axis=0)
    window = jnp.dot(window_embed, projection, preferred_element_type=jnp.float32).astype(
        jnp.bfloat16
    )
    window = lax.optimization_barrier(window).astype(jnp.float32)

    def forward_block(pair):
        dense = margin_block(pair[0], pair[1], slots)
        return jnp.dot(dense, window, precision=lax.Precision.HIGHEST)

    forcing = lax.map(forward_block, (index_blocks, weight_blocks)).reshape(height, width, channels)
    field = ocean_state.astype(jnp.float32) + forcing
    widened = with_halo(field, (("lon", 1),), 3)
    padded = clear_ends(with_halo(widened, (("lat", 0),), 3))
    conv_out = depthwise(padded, dw_kernel)
    normed, sigma = norm_forward(conv_out)
    ln_cells = (normed * norm_gain).astype(jnp.bfloat16)
    g_out = cotangent.astype(jnp.float32)
    gy_cells = (sea_mask.astype(jnp.float32)[..., None] * g_out).astype(jnp.bfloat16)
    g_ln, grad_in, grad_out = mlp_back(
        ln_cells.reshape(-1, channels), gy_cells.reshape(-1, channels), w_in, w_out
    )
    g_conv, grad_gain = norm_back(g_ln.reshape(height, width, channels), normed, sigma, norm_gain)
    grad_kernel = kernel_grad(g_conv, padded)
    g_widened = with_halo(g_conv.astype(jnp.bfloat16), (("lon", 1),), 3).astype(g_conv.dtype)
    g_padded = clear_ends(
        with_halo(g_widened.astype(jnp.bfloat16), (("lat", 0),), 3).astype(g_widened.dtype)
    )
    grad_state = g_out + depthwise_back(g_padded, dw_kernel)
    state_blocks = grad_state.reshape(blocks, group, channels)

    def backward_block(total, triple):
        dense = margin_block(triple[0], triple[1], slots)
        added = lax.dot_general(
            dense,
            triple[2],
            (((0,), (0,)), ((), ())),
            precision=lax.Precision.HIGHEST,
            preferred_element_type=jnp.float32,
        )
        return (total + added, None)

    g_window, unused = lax.scan(
        backward_block,
        jnp.zeros((slots, channels), jnp.float32),
        (index_blocks, weight_blocks, state_blocks),
    )
    g_window_embed = jnp.dot(
        g_window, projection.astype(jnp.float32).T, precision=lax.Precision.HIGHEST
    )
    returned = shifted(g_window_embed[cells_atm:].astype(jnp.bfloat16), "lat", 1).astype(
        jnp.float32
    )
    grad_embed = g_window_embed[:cells_atm] + returned
    grad_projection = jnp.dot(
        window_embed.astype(jnp.float32).T, g_window, precision=lax.Precision.HIGHEST
    )
    partials = (grad_projection, grad_kernel, grad_gain, grad_in, grad_out)
    totals = lax.psum(
        (partials[0], partials[1], partials[2], partials[3], partials[4]), ("lat", "lon")
    )
    return (grad_state, grad_embed, totals[0], totals[1], totals[2], totals[3], totals[4])


def solution(mesh):
    return jax.shard_map(
        shards,
        mesh=mesh,
        in_specs=(
            P("lat", "lon", None),
            P("lat", "lon", None),
            P(("lat", "lon"), None),
            P(),
            P(),
            P(),
            P(),
            P(),
            P(None, "lat", "lon"),
            P(None, "lat", "lon"),
            P("lat", "lon"),
        ),
        out_specs=(P("lat", "lon", None), P(("lat", "lon"), None), P(), P(), P(), P(), P()),
        check_vma=False,
    )
```

profile of v0, /device:TPU:1, one launch (start us, length us, event | category | flops | bytes accessed | tf_op | source)
XLA Modules:
  0.0 303.8 jit_solution(2840815184658373057)
XLA Ops:
  7.2 3.3 %collective-permute-start = (bf16[512,256]{1,0:T(8,128)(2,1)}, bf16[512,256]{1,0:T(8,128)(2,1)S(1)}, u32[]{:S(2)}, u32[]{:S(2)}) collective-permute-start(bf16[512,256]{1,0:T(8,128)(2,1)} %param.17), channel_id=1, source_target_pairs={{8,0},{16,8},{24,16},{32,24},{40,32},{48,40},{56,48},{64,56},{72,6... | collective-permute-start | bytes 786440 | tf_op jit(solution)/shard_map/ppermute | solution.py:12
  10.5 1.0 constant_dynamic-update-slice_fusion.1
  11.5 1.0 slice_bitcast_fusion.48
  12.5 3.5 %collective-permute-done = bf16[512,256]{1,0:T(8,128)(2,1)S(1)} collective-permute-done((bf16[512,256]{1,0:T(8,128)(2,1)}, bf16[512,256]{1,0:T(8,128)(2,1)S(1)}, u32[]{:S(2)}, u32[]{:S(2)}) %collective-permute-start) | collective-permute-done | bytes 262176 | tf_op jit(solution)/shard_map/ppermute | solution.py:12
  16.0 1.2 convolution_convert_fusion
  17.3 17.9 %while.21 = (s32[]{:T(128)}, f32[3,768,128]{2,1,0:T(8,128)S(1)}, s32[3,4,768]{2,1,0:T(4,128)S(1)}, f32[3,4,768]{2,1,0:T(4,128)S(1)}, f32[1024,128]{1,0:T(8,128)S...) while((s32[]{:T(128)}, f32[3,768,128]{2,1,0:T(8,128)S(1)}, s32[3,4,768]{2,1,0:T(4,128)S(1)}, ...), condition=%wide.region_1.2_spmd, body=%wide.region_0.1_spmd.sunk | while | flops 1216610304 | bytes 999605 | solution.py:174
  17.4 5.8 %fusion.140 = f32[3,768,128]{2,1,0:T(8,128)S(1)} fusion(f32[3,768,128]{2,1,0:T(8,128)S(1)} %get-tuple-element.341, s32[]{:T(128)S(6)} %copy.22, f32[1024,128]{1,0:T(8,128)S(1)} %get-tuple-element.354, f32[768]{0:T(1024)S(1)} %get-tuple-element.309, s32[768]{0:T(1024)S(1)} %get-tuple-element.310, f32[768]{0:T(1024)S(1)} %get-tuple-element.311, ...), kind=kOutput, calls=%fused_computation.22.clone.1 | convolution fusion | flops 1216610304 | bytes 950276 | tf_op jit(solution)/shard_map/while/body/eval_jaxpr/dot_general | solution.py:172
  23.4 5.8 %fusion.140 = f32[3,768,128]{2,1,0:T(8,128)S(1)} fusion(f32[3,768,128]{2,1,0:T(8,128)S(1)} %get-tuple-element.341, s32[]{:T(128)S(6)} %copy.22, f32[1024,128]{1,0:T(8,128)S(1)} %get-tuple-element.354, f32[768]{0:T(1024)S(1)} %get-tuple-element.309, s32[768]{0:T(1024)S(1)} %get-tuple-element.310, f32[768]{0:T(1024)S(1)} %get-tuple-element.311, ...), kind=kOutput, calls=%fused_computation.22.clone.1 | convolution fusion | flops 1216610304 | bytes 950276 | tf_op jit(solution)/shard_map/while/body/eval_jaxpr/dot_general | solution.py:172
  29.3 5.8 %fusion.140 = f32[3,768,128]{2,1,0:T(8,128)S(1)} fusion(f32[3,768,128]{2,1,0:T(8,128)S(1)} %get-tuple-element.341, s32[]{:T(128)S(6)} %copy.22, f32[1024,128]{1,0:T(8,128)S(1)} %get-tuple-element.354, f32[768]{0:T(1024)S(1)} %get-tuple-element.309, s32[768]{0:T(1024)S(1)} %get-tuple-element.310, f32[768]{0:T(1024)S(1)} %get-tuple-element.311, ...), kind=kOutput, calls=%fused_computation.22.clone.1 | convolution fusion | flops 1216610304 | bytes 950276 | tf_op jit(solution)/shard_map/while/body/eval_jaxpr/dot_general | solution.py:172
  35.2 1.2 convert_add_fusion.1
  36.4 1.4 collective-permute-start.1
  37.8 3.5 %collective-permute-start.2 = (f32[9,3,128]{2,1,0:T(4,128)S(1)}, f32[9,3,128]{2,1,0:T(4,128)S(1)}, u32[]{:S(2)}, u32[]{:S(2)}) collective-permute-start(f32[9,3,128]{2,1,0:T(4,128)S(1)} %get-tuple-element.180), channel_id=1, source_target_pairs={{1,0},{2,1},{3,2},{4,3},{5,4},{6,5},{7,6},{0,7},{9,8},{10,9},{11,1... | collective-permute-start | bytes 41480 | tf_op jit(solution)/shard_map/ppermute | solution.py:24
  42.5 0.9 collective-permute-start.3
  44.7 3.5 %collective-permute-done.3 = f32[3,262,128]{2,1,0:T(8,128)S(1)} collective-permute-done((f32[3,262,128]{2,1,0:T(8,128)S(1)}, f32[3,262,128]{2,1,0:T(8,128)S(1)}, u32[]{:S(2)}, u32[]{:S(2)}) %collective-permute-start.3) | collective-permute-done | bytes 402464 | tf_op jit(solution)/shard_map/ppermute | solution.py:21
  48.2 0.7 copy-done.20
  48.9 1.8 collective-permute-done.4
  50.8 1.3 maximum_multiply_fusion
  52.4 8.4 %fusion.109 = (f32[9,256]{1,0:T(8,128)S(1)}, f32[9,256,128]{2,1,0:T(8,128)S(1)}) fusion(f32[128]{0:T(128)S(1)} %copy-done.81, f32[15,262,128]{2,1,0:T(8,128)S(1)} %maximum_multiply_fusion, f32[128]{0:T(128)S(1)} %copy-done.83, f32[128]{0:T(128)S(1)} %get-tuple-element.186, f32[128]{0:T(128)S(1)} %get-tuple-element.187, f32[128]{0:T(128)S(1)} %get-tuple-element.188, ...), kind=kLoop, calls=%fused_computation.306 | loop fusion | flops 28899072 | bytes 59016704 | tf_op jit(solution)/shard_map/reduce_sum | solution.py:73
  61.6 0.8 multiply_convert_fusion.2
  62.4 0.8 fusion.112
  63.5 3.5 %fusion.54 = bf16[2304,512]{1,0:T(8,128)(2,1)S(1)} fusion(f32[2304,512]{1,0:T(8,128)S(1)} %fusion.112, bf16[2304,128]{1,0:T(8,128)(2,1)S(1)} %bitcast.196, bf16[512,128]{1,0:T(8,128)(2,1)S(1)} %copy-done.124), kind=kOutput, calls=%fused_computation.74 | convolution fusion | flops 325582848 | bytes 7798784 | tf_op jit(solution)/shard_map/dot_general | solution.py:100
  67.0 1.8 multiply_reduce_fusion.51
  68.8 2.9 multiply_reduce_fusion
  71.7 4.1 %multiply_reduce_fusion.1 = (f32[128]{0:T(128)}, f32[128]{0:T(128)}, f32[128]{0:T(128)}, f32[128]{0:T(128)}, f32[128]{0:T(128)}, /*index=5*/f32[128]{0:T(128)}, ...) fusion(f32[15,262,128]{2,1,0:T(8,128)S(1)} %maximum_multiply_fu, ...), kind=kLoop, calls=%fused_computation.181 | loop fusion | flops 12678912 | bytes 24819200 | tf_op jit(solution)/shard_map/reduce_sum | solution.py:64
  75.8 3.3 %multiply_reduce_fusion.19 = (f32[128]{0:T(128)}, f32[128]{0:T(128)}, f32[128]{0:T(128)}, f32[128]{0:T(128)}, f32[128]{0:T(128)}, /*index=5*/f32[128]{0:T(128)},...) fusion(f32[9,256,128]{2,1,0:T(8,128)S(1)} %get-tuple-element.17, ...), kind=kLoop, calls=%fused_computation.199 | loop fusion | flops 10909440 | bytes 23012352 | tf_op jit(solution)/shard_map/reduce_sum | solution.py:64
  79.2 1.0 collective-permute-start.5
  80.2 3.0 %collective-permute-start.6 = (bf16[9,3,128]{2,1,0:T(4,128)(2,1)S(1)}, bf16[9,3,128]{2,1,0:T(4,128)(2,1)S(1)}, u32[]{:S(2)}, u32[]{:S(2)}) collective-permute-start(bf16[9,3,128]{2,1,0:T(4,128)(2,1)S(1)} %get-tuple-element.184), channel_id=1, source_target_pairs={{1,0},{2,1},{3,2},{4,3},{5,4},{6,5},{7,6},{0,7},{9,8},{10,9},{11,1... | collective-permute-start | bytes 20744 | tf_op jit(solution)/shard_map/ppermute | solution.py:24
  83.3 2.4 fusion.55
  85.8 1.0 collective-permute-start.7
  87.1 1.2 fusion.115
  88.6 0.8 collective-permute-done.7
  89.4 2.5 collective-permute-done.8
  92.5 8.9 %convert_add_fusion = f32[9,256,128]{2,1,0:T(8,128)} fusion(bf16[9,256,128]{2,1,0:T(8,128)(2,1)S(1)} %copy-done.13, f32[15,262,128]{2,1,0:T(8,128)S(1)} %convert_multiply_fusion, f32[128]{0:T(128)S(1)} %copy-done.82, f32[128]{0:T(128)S(1)} %copy-done.84, f32[128]{0:T(128)S(1)} %get-tuple-element.186, f32[128]{0:T(128)S(1)} %get-tuple-element.187, ...), kind=kLoop, calls=%fused_computation.79 | loop fusion | flops 29196288 | bytes 59597312 | tf_op jit(solution)/shard_map/add | solution.py:192
  101.4 23.0 %while.22 = (s32[]{:T(128)}, f32[1024,128]{1,0:T(8,128)S(1)}, s32[3,4,768]{2,1,0:T(4,128)S(1)}, f32[3,4,768]{2,1,0:T(4,128)S(1)}, f32[3,768,128]{2,1,0:T(8,128)}, /*index=5*/s32[]{:T(128)}, s32[]{:T(128)}, s32[]{}, s32[]{}, s32[]{}) while((s32[]{:T(128)}, f32[1024,128]{1,0:T(8,128)S(1)}, s32[3,4,768]{2,1,0:T(4,128)S(1)}, ...), condition=%wide.region_7.8_spmd.clone, body=%wide.region_6.7_spmd.clone.sunk | while | flops 1216872448 | bytes 1515711 | solution.py:206
  101.5 7.6 %fusion.143 = f32[1024,128]{1,0:T(8,128)S(1)} fusion(f32[768]{0:T(1024)S(1)} %get-tuple-element.322, s32[768]{0:T(1024)S(1)} %get-tuple-element.323, f32[768]{0:T(1024)S(1)} %get-tuple-element.324, s32[768]{0:T(1024)S(1)} %get-tuple-element.325, f32[768]{0:T(1024)S(1)} %get-tuple-element.326, s32[768]{0:T(1024)S(1)} %get-tuple-element.327, ...), kind=kOutput, calls=%fused_computation.53.clone.1 | convolution fusion | flops 1216872448 | bytes 1466373 | tf_op jit(solution)/shard_map/while/body/eval_jaxpr/dot_general | solution.py:197
  109.2 7.5 %fusion.143 = f32[1024,128]{1,0:T(8,128)S(1)} fusion(f32[768]{0:T(1024)S(1)} %get-tuple-element.322, s32[768]{0:T(1024)S(1)} %get-tuple-element.323, f32[768]{0:T(1024)S(1)} %get-tuple-element.324, s32[768]{0:T(1024)S(1)} %get-tuple-element.325, f32[768]{0:T(1024)S(1)} %get-tuple-element.326, s32[768]{0:T(1024)S(1)} %get-tuple-element.327, ...), kind=kOutput, calls=%fused_computation.53.clone.1 | convolution fusion | flops 1216872448 | bytes 1466373 | tf_op jit(solution)/shard_map/while/body/eval_jaxpr/dot_general | solution.py:197
  116.9 7.5 %fusion.143 = f32[1024,128]{1,0:T(8,128)S(1)} fusion(f32[768]{0:T(1024)S(1)} %get-tuple-element.322, s32[768]{0:T(1024)S(1)} %get-tuple-element.323, f32[768]{0:T(1024)S(1)} %get-tuple-element.324, s32[768]{0:T(1024)S(1)} %get-tuple-element.325, f32[768]{0:T(1024)S(1)} %get-tuple-element.326, s32[768]{0:T(1024)S(1)} %get-tuple-element.327, ...), kind=kOutput, calls=%fused_computation.53.clone.1 | convolution fusion | flops 1216872448 | bytes 1466373 | tf_op jit(solution)/shard_map/while/body/eval_jaxpr/dot_general | solution.py:197
  124.5 1.4 fusion.114
  125.8 1.7 fusion.113
  127.6 1.0 copy-done.11
  129.3 2.2 collective-permute-start.9
  131.9 2.0 multiply_reduce_fusion.37
  134.4 79.5 %all-reduce = (f32[7,7,128]{2,1,0:T(8,128)}, f32[128]{0:T(128)}) all-reduce(f32[7,7,128]{2,1,0:T(8,128)S(1)} %reshape.131, f32[128]{0:T(128)S(1)} %copy-done.103), channel_id=1, replica_groups=mesh['lat'=16,'lon'=8] {'lat','lon'}, use_global_device_ids=true, to_apply=%region_58.59 | all-reduce | flops 6400 | bytes 51200 | tf_op jit(solution)/shard_map/psum | solution.py:222
  214.0 2.0 slice_add_fusion
  215.9 76.1 %all-reduce.4.cloned.1.call-done = (f32[256,128]{1,0:T(8,128)}, f32[128,512]{1,0:T(8,128)}, f32[512,128]{1,0:T(8,128)}) async-done(((f32[256,128]{1,0:T(8,128)}, f32[128,512]{1,0:T(8,128)}, f32[512,128]{1,0:T(8,128)}), (f32[256,128]{1,0:T(8,128)}, f32[128,512]{1,0:T(8,128)}, f32[512,128]{1,0:T(8,128)})) %all-reduce.4.cloned.1.call-update) | async-done | bytes 655376 | tf_op jit(solution)/shard_map/psum | solution.py:222
  292.0 1.6 copy.35
  293.6 1.7 copy.36
  295.3 1.7 copy.37
  (297 shorter events, 6.0 us)
Async XLA Ops:
  7.2 55.2 %copy-start = (bf16[128,512]{1,0:T(8,128)(2,1)S(1)}, bf16[128,512]{1,0:T(8,128)(2,1)}, u32[]{:S(2)}) copy-start(bf16[128,512]{1,0:T(8,128)(2,1)} %param.21) | copy-start | bytes 393220
  7.2 284.9 %all-reduce.4.cloned.1.call-start = ((), (), s32[]{:S(2)}) async-start(), calls=%async_computation | async-start | bytes 1310720 | tf_op jit(solution)/shard_map/psum | solution.py:222
  7.2 8.8 %collective-permute-start = (bf16[512,256]{1,0:T(8,128)(2,1)}, bf16[512,256]{1,0:T(8,128)(2,1)S(1)}, u32[]{:S(2)}, u32[]{:S(2)}) collective-permute-start(bf16[512,256]{1,0:T(8,128)(2,1)} %param.17), channel_id=1, source_target_pairs={{8,0},{16,8},{24,16},{32,24},{40,32},{48,40},{56,48},{64,56},{72,6... | collective-permute-start | bytes 786440 | tf_op jit(solution)/shard_map/ppermute | solution.py:12
  36.4 6.0 %collective-permute-start.1 = (f32[9,3,128]{2,1,0:T(4,128)S(1)}, f32[9,3,128]{2,1,0:T(4,128)S(1)}, u32[]{:S(2)}, u32[]{:S(2)}) collective-permute-start(f32[9,3,128]{2,1,0:T(4,128)S(1)} %get-tuple-element.179), channel_id=1, source_target_pairs={{0,1},{1,2},{2,3},{3,4},{4,5},{5,6},{6,7},{7,0},{8,9},{9,10},{10,1... | collective-permute-start | bytes 41480 | tf_op jit(solution)/shard_map/ppermute | solution.py:21
  37.8 4.6 %collective-permute-start.2 = (f32[9,3,128]{2,1,0:T(4,128)S(1)}, f32[9,3,128]{2,1,0:T(4,128)S(1)}, u32[]{:S(2)}, u32[]{:S(2)}) collective-permute-start(f32[9,3,128]{2,1,0:T(4,128)S(1)} %get-tuple-element.180), channel_id=1, source_target_pairs={{1,0},{2,1},{3,2},{4,3},{5,4},{6,5},{7,6},{0,7},{9,8},{10,9},{11,1... | collective-permute-start | bytes 41480 | tf_op jit(solution)/shard_map/ppermute | solution.py:24
  42.0 10.2 %copy-start.25 = (f32[128]{0:T(128)}, f32[128]{0:T(128)S(1)}, u32[]{:S(2)}) copy-start(f32[128]{0:T(128)S(1)} %get-tuple-element.204) | copy-start | bytes 1540
  42.0 10.2 %copy-start.27 = (f32[128]{0:T(128)}, f32[128]{0:T(128)S(1)}, u32[]{:S(2)}) copy-start(f32[128]{0:T(128)S(1)} %get-tuple-element.205) | copy-start | bytes 1540
  42.5 5.7 %collective-permute-start.3 = (f32[3,262,128]{2,1,0:T(8,128)S(1)}, f32[3,262,128]{2,1,0:T(8,128)S(1)}, u32[]{:S(2)}, u32[]{:S(2)}) collective-permute-start(f32[3,262,128]{2,1,0:T(8,128)S(1)} %get-tuple-element.176), channel_id=1, source_target_pairs={{0,8},{8,16},{16,24},{24,32},{32,40},{40,48},{48,56},{56,64},{64,7... | collective-permute-start | bytes 1207304 | tf_op jit(solution)/shard_map/ppermute | solution.py:21
  43.3 7.4 %collective-permute-start.4 = (f32[3,262,128]{2,1,0:T(8,128)S(1)}, f32[3,262,128]{2,1,0:T(8,128)}, u32[]{:S(2)}, u32[]{:S(2)}) collective-permute-start(f32[3,262,128]{2,1,0:T(8,128)S(1)} %get-tuple-element.177), channel_id=1, source_target_pairs={{8,0},{16,8},{24,16},{32,24},{40,32},{48,40},{56,48},{64,56},{72,6... | collective-permute-start | bytes 1207304 | tf_op jit(solution)/shard_map/ppermute | solution.py:24
  44.0 8.1 %copy-start.122 = (f32[15]{0:T(128)}, f32[15]{0:T(128)S(1)}, u32[]{:S(2)}) copy-start(f32[15]{0:T(128)S(1)} %or_select_fusion) | copy-start | bytes 184
  44.4 18.9 %copy-start.16 = (bf16[9,256,128]{2,1,0:T(8,128)(2,1)}, bf16[9,256,128]{2,1,0:T(8,128)(2,1)S(1)}, u32[]{:S(2)}) copy-start(bf16[9,256,128]{2,1,0:T(8,128)(2,1)S(1)} %fusion.56) | copy-start | bytes 1769476
  44.4 7.7 %copy-start.29 = (f32[128]{0:T(128)S(1)}, f32[128]{0:T(128)}, u32[]{:S(2)}) copy-start(f32[128]{0:T(128)} %get-tuple-element.206) | copy-start | bytes 1540
  44.4 7.7 %copy-start.31 = (f32[128]{0:T(128)S(1)}, f32[128]{0:T(128)}, u32[]{:S(2)}) copy-start(f32[128]{0:T(128)} %get-tuple-element.207) | copy-start | bytes 1540
  44.4 7.7 %copy-start.33 = (f32[128]{0:T(128)S(1)}, f32[128]{0:T(128)}, u32[]{:S(2)}) copy-start(f32[128]{0:T(128)} %get-tuple-element.208) | copy-start | bytes 1540
  44.4 7.7 %copy-start.35 = (f32[128]{0:T(128)S(1)}, f32[128]{0:T(128)}, u32[]{:S(2)}) copy-start(f32[128]{0:T(128)} %get-tuple-element.209) | copy-start | bytes 1540
  44.5 7.7 %copy-start.37 = (f32[128]{0:T(128)S(1)}, f32[128]{0:T(128)}, u32[]{:S(2)}) copy-start(f32[128]{0:T(128)} %get-tuple-element.210) | copy-start | bytes 1540
  44.5 7.7 %copy-start.39 = (f32[128]{0:T(128)S(1)}, f32[128]{0:T(128)}, u32[]{:S(2)}) copy-start(f32[128]{0:T(128)} %get-tuple-element.211) | copy-start | bytes 1540
  44.5 7.7 %copy-start.41 = (f32[128]{0:T(128)S(1)}, f32[128]{0:T(128)}, u32[]{:S(2)}) copy-start(f32[128]{0:T(128)} %get-tuple-element.212) | copy-start | bytes 1540
  44.5 7.7 %copy-start.43 = (f32[128]{0:T(128)S(1)}, f32[128]{0:T(128)}, u32[]{:S(2)}) copy-start(f32[128]{0:T(128)} %get-tuple-element.213) | copy-start | bytes 1540
  44.5 7.7 %copy-start.45 = (f32[128]{0:T(128)S(1)}, f32[128]{0:T(128)}, u32[]{:S(2)}) copy-start(f32[128]{0:T(128)} %get-tuple-element.214) | copy-start | bytes 1540
  44.5 7.7 %copy-start.47 = (f32[128]{0:T(128)S(1)}, f32[128]{0:T(128)}, u32[]{:S(2)}) copy-start(f32[128]{0:T(128)} %get-tuple-element.215) | copy-start | bytes 1540
  44.5 7.7 %copy-start.49 = (f32[128]{0:T(128)S(1)}, f32[128]{0:T(128)}, u32[]{:S(2)}) copy-start(f32[128]{0:T(128)} %get-tuple-element.216) | copy-start | bytes 1540
  44.5 7.7 %copy-start.51 = (f32[128]{0:T(128)S(1)}, f32[128]{0:T(128)}, u32[]{:S(2)}) copy-start(f32[128]{0:T(128)} %get-tuple-element.217) | copy-start | bytes 1540
  44.5 7.7 %copy-start.53 = (f32[128]{0:T(128)S(1)}, f32[128]{0:T(128)}, u32[]{:S(2)}) copy-start(f32[128]{0:T(128)} %get-tuple-element.218) | copy-start | bytes 1540
  44.5 7.7 %copy-start.55 = (f32[128]{0:T(128)S(1)}, f32[128]{0:T(128)}, u32[]{:S(2)}) copy-start(f32[128]{0:T(128)} %get-tuple-element.219) | copy-start | bytes 1540
  44.6 7.7 %copy-start.57 = (f32[128]{0:T(128)S(1)}, f32[128]{0:T(128)}, u32[]{:S(2)}) copy-start(f32[128]{0:T(128)} %get-tuple-element.220) | copy-start | bytes 1540
  44.6 7.7 %copy-start.59 = (f32[128]{0:T(128)S(1)}, f32[128]{0:T(128)}, u32[]{:S(2)}) copy-start(f32[128]{0:T(128)} %get-tuple-element.221) | copy-start | bytes 1540
  44.6 7.7 %copy-start.61 = (f32[128]{0:T(128)S(1)}, f32[128]{0:T(128)}, u32[]{:S(2)}) copy-start(f32[128]{0:T(128)} %get-tuple-element.222) | copy-start | bytes 1540
  44.6 7.7 %copy-start.63 = (f32[128]{0:T(128)S(1)}, f32[128]{0:T(128)}, u32[]{:S(2)}) copy-start(f32[128]{0:T(128)} %get-tuple-element.223) | copy-start | bytes 1540
  44.6 7.7 %copy-start.65 = (f32[128]{0:T(128)S(1)}, f32[128]{0:T(128)}, u32[]{:S(2)}) copy-start(f32[128]{0:T(128)} %get-tuple-element.224) | copy-start | bytes 1540
  44.6 7.7 %copy-start.67 = (f32[128]{0:T(128)S(1)}, f32[128]{0:T(128)}, u32[]{:S(2)}) copy-start(f32[128]{0:T(128)} %get-tuple-element.225) | copy-start | bytes 1540
  44.6 7.7 %copy-start.69 = (f32[128]{0:T(128)S(1)}, f32[128]{0:T(128)}, u32[]{:S(2)}) copy-start(f32[128]{0:T(128)} %get-tuple-element.226) | copy-start | bytes 1540
  44.6 7.7 %copy-start.71 = (f32[128]{0:T(128)S(1)}, f32[128]{0:T(128)}, u32[]{:S(2)}) copy-start(f32[128]{0:T(128)} %get-tuple-element.227) | copy-start | bytes 1540
  44.6 7.7 %copy-start.73 = (f32[128]{0:T(128)S(1)}, f32[128]{0:T(128)}, u32[]{:S(2)}) copy-start(f32[128]{0:T(128)} %get-tuple-element.228) | copy-start | bytes 1540
  44.7 7.7 %copy-start.75 = (f32[128]{0:T(128)S(1)}, f32[128]{0:T(128)}, u32[]{:S(2)}) copy-start(f32[128]{0:T(128)} %get-tuple-element.229) | copy-start | bytes 1540
  44.7 7.7 %copy-start.77 = (f32[128]{0:T(128)S(1)}, f32[128]{0:T(128)}, u32[]{:S(2)}) copy-start(f32[128]{0:T(128)} %get-tuple-element.230) | copy-start | bytes 1540
  44.7 7.7 %copy-start.79 = (f32[128]{0:T(128)S(1)}, f32[128]{0:T(128)}, u32[]{:S(2)}) copy-start(f32[128]{0:T(128)} %get-tuple-element.231) | copy-start | bytes 1540
  44.7 7.7 %copy-start.81 = (f32[128]{0:T(128)S(1)}, f32[128]{0:T(128)}, u32[]{:S(2)}) copy-start(f32[128]{0:T(128)} %get-tuple-element.232) | copy-start | bytes 1540
  44.7 7.7 %copy-start.83 = (f32[128]{0:T(128)S(1)}, f32[128]{0:T(128)}, u32[]{:S(2)}) copy-start(f32[128]{0:T(128)} %get-tuple-element.233) | copy-start | bytes 1540
  68.8 14.4 %slice-start = ((s8[4718592]{0:T(1024)(128)(4,1)}), s8[4194304]{0:T(1024)(128)(4,1)S(1)}, s32[]{:S(2)}) async-start(s8[4718592]{0:T(1024)(128)(4,1)} %bitcast.191), calls=%async_computation.1 | async-start | bytes 8388608
  71.7 11.5 %slice-start.1 = ((s8[4718592]{0:T(1024)(128)(4,1)}), s8[524288]{0:T(1024)(128)(4,1)S(1)}, s32[]{:S(2)}) async-start(s8[4718592]{0:T(1024)(128)(4,1)} %bitcast.191), calls=%async_computation.2 | async-start | bytes 1048576
  79.2 6.5 %collective-permute-start.5 = (bf16[9,3,128]{2,1,0:T(4,128)(2,1)S(1)}, bf16[9,3,128]{2,1,0:T(4,128)(2,1)S(1)}, u32[]{:S(2)}, u32[]{:S(2)}) collective-permute-start(bf16[9,3,128]{2,1,0:T(4,128)(2,1)S(1)} %get-tuple-element.183), channel_id=1, source_target_pairs={{0,1},{1,2},{2,3},{3,4},{4,5},{5,6},{6,7},{7,0},{8,9},{9,10},{10,1... | collective-permute-start | bytes 20744 | tf_op jit(solution)/shard_map/ppermute | solution.py:21
  80.2 5.4 %collective-permute-start.6 = (bf16[9,3,128]{2,1,0:T(4,128)(2,1)S(1)}, bf16[9,3,128]{2,1,0:T(4,128)(2,1)S(1)}, u32[]{:S(2)}, u32[]{:S(2)}) collective-permute-start(bf16[9,3,128]{2,1,0:T(4,128)(2,1)S(1)} %get-tuple-element.184), channel_id=1, source_target_pairs={{1,0},{2,1},{3,2},{4,3},{5,4},{6,5},{7,6},{0,7},{9,8},{10,9},{11,1... | collective-permute-start | bytes 20744 | tf_op jit(solution)/shard_map/ppermute | solution.py:24
  85.8 3.7 %collective-permute-start.7 = (bf16[3,262,128]{2,1,0:T(8,128)(2,1)S(1)}, bf16[3,262,128]{2,1,0:T(8,128)(2,1)S(1)}, u32[]{:S(2)}, u32[]{:S(2)}) collective-permute-start(bf16[3,262,128]{2,1,0:T(8,128)(2,1)S(1)} %get-tuple-element.181), channel_id=1, source_target_pairs={{0,8},{8,16},{16,24},{24,32},{32,40},{40,48},{48,56},{56,64},{64,7... | collective-permute-start | bytes 603656 | tf_op jit(solution)/shard_map/ppermute | solution.py:21
  86.8 5.2 %collective-permute-start.8 = (bf16[3,262,128]{2,1,0:T(8,128)(2,1)S(1)}, bf16[3,262,128]{2,1,0:T(8,128)(2,1)S(1)}, u32[]{:S(2)}, u32[]{:S(2)}) collective-permute-start(bf16[3,262,128]{2,1,0:T(8,128)(2,1)S(1)} %get-tuple-element.182), channel_id=1, source_target_pairs={{8,0},{16,8},{24,16},{32,24},{40,32},{48,40},{56,48},{64,56},{72,6... | collective-permute-start | bytes 603656 | tf_op jit(solution)/shard_map/ppermute | solution.py:24
  92.5 9.0 %copy-start.14 = (f32[1024,128]{1,0:T(8,128)S(1)}, f32[1024,128]{1,0:T(8,128)}, u32[]{:S(2)}) copy-start(f32[1024,128]{1,0:T(8,128)} %custom-call) | copy-start | bytes 1572868
  101.4 23.0 %copy-start.10 = (bf16[1024,256]{1,0:T(8,128)(2,1)S(1)}, bf16[1024,256]{1,0:T(8,128)(2,1)}, u32[]{:S(2)}) copy-start(bf16[1024,256]{1,0:T(8,128)(2,1)} %copy-done.9) | copy-start | bytes 1572868
  129.3 84.7 %collective-permute-start.9 = (bf16[512,256]{1,0:T(8,128)(2,1)}, bf16[512,256]{1,0:T(8,128)(2,1)}, u32[]{:S(2)}, u32[]{:S(2)}) collective-permute-start(bf16[512,256]{1,0:T(8,128)(2,1)} %slice.1295), channel_id=1, source_target_pairs={{0,8},{8,16},{16,24},{24,32},{32,40},{40,48},{48,56},{56,64},{64,7... | collective-permute-start | bytes 786440 | tf_op jit(solution)/shard_map/ppermute | solution.py:12
  (90 other events, 284.9 us)
Sparse Core Ops, SparseCore 0:
  131.6 160.3 all-reduce.3
where the time goes:
time: 304 us
  waiting for transfers between devices  88.6 us (29%)
  blocking collectives  79.5 us (26%)
  matrix products  54 us (18%)
  other arithmetic  36.5 us (12%)
  starting transfers between devices  16.7 us (5%)
  between operations  16 us (5%)
  local copies, waits for them, and re-layouts  12.2 us (4%)
    psum x1, blocking collectives, shards(): lax.psum((partials[0], partials[1], partials[2], partials[3], partials[4]...  79.5 us
    psum x1, waiting for transfers between devices, shards(): lax.psum((partials[0], partials[1], partials[2], partials[3], partials[4]...  76.1 us
    dot_general x3, matrix products, backward_block(): lax.dot_general(dense, triple[2], (((0,), (0,)), ((), ())), precision=lax...  22.6 us
    dot_general x3, matrix products, forward_block(): return jnp.dot(dense, window, precision=lax.Precision.HIGHEST)  17.5 us
    reduce_sum x3, other arithmetic, kernel_grad(): jnp.sum(grad * padded[row_tap:row_tap + height, col_tap:col_tap + width],...  9.44 us
    add x1, other arithmetic, shards(): grad_state = g_out + depthwise_back(g_padded, dw_kernel)  8.94 us
    unnamed x258, local copies, waits for them, and re-layouts  8.46 us
    reduce_sum x1, other arithmetic, norm_forward(): center = field - jnp.mean(field, axis=-1, keepdims=True)  8.39 us
  transfers between devices with their start and end apart: 11, of which 7 were waited for; matrix products, arithmetic and copies ran while one was open for 4% of the time, Pallas kernels for 0%

commit v1 on v0

--- a/solution.py
+++ b/solution.py
@@ -1,6 +1,9 @@
+import functools
 import jax
 import jax.numpy as jnp
 from jax import lax
+from jax.experimental import pallas as pl
+from jax.experimental.pallas import tpu as pltpu
 from jax.sharding import PartitionSpec as P
 
 EPSILON = 1e-05
@@ -135,6 +138,122 @@
         if height % count == 0 and count <= limit:
             best = count
     return best
+
+
+ROWS = 16
+STRIDE = 55
+
+
+def all_sum_kernel(
+    pieces, inverse, x_ref, o_ref, send, recv, send_sem, recv_sem, out_send_sem, out_recv_sem
+):
+    lons = lax.axis_size("lon")
+    total = lax.axis_size("lat") * lons
+    me = lax.axis_index("lat") * lons + lax.axis_index("lon")
+    mine = (me * inverse) % total
+
+    def place(device):
+        return {"lat": device // lons, "lon": device % lons}
+
+    def rows_of(piece):
+        return pl.ds(pl.multiple_of(piece * ROWS, ROWS), ROWS)
+
+    barrier = pltpu.get_barrier_semaphore()
+
+    def greet(step, carry):
+        pl.semaphore_signal(
+            barrier,
+            inc=1,
+            device_id=place((me + step) % total),
+            device_id_type=pl.DeviceIdType.MESH,
+        )
+        return carry
+
+    lax.fori_loop(1, total, greet, 0)
+    pl.semaphore_wait(barrier, total - 1)
+
+    def scatter(piece, carry):
+        owner = (piece * STRIDE) % total
+
+        @pl.when(owner != me)
+        def _():
+            slot = (me - owner + total) % total - 1
+            pltpu.make_async_remote_copy(
+                src_ref=x_ref.at[rows_of(piece)],
+                dst_ref=recv.at[rows_of(slot)],
+                send_sem=send_sem,
+                recv_sem=recv_sem,
+                device_id=place(owner),
+                device_id_type=pl.DeviceIdType.MESH,
+            ).start()
+
+        return carry
+
+    lax.fori_loop(0, pieces, scatter, 0)
+
+    @pl.when(mine < pieces)
+    def _():
+        pltpu.make_async_copy(recv, recv, recv_sem).wait()
+        own = x_ref[rows_of(mine)].astype(jnp.float32)
+        others = recv[...].astype(jnp.float32).reshape(total - 1, ROWS, 128)
+        send[...] = (own + jnp.sum(others, axis=0)).astype(jnp.bfloat16)
+        o_ref[rows_of(mine)] = send[...]
+
+        def gather(step, carry):
+            pltpu.make_async_remote_copy(
+                src_ref=send,
+                dst_ref=o_ref.at[rows_of(mine)],
+                send_sem=out_send_sem,
+                recv_sem=out_recv_sem,
+                device_id=place((me + step) % total),
+                device_id_type=pl.DeviceIdType.MESH,
+            ).start()
+            return carry
+
+        lax.fori_loop(1, total, gather, 0)
+        part = x_ref.at[pl.ds(0, (pieces - 1) * ROWS)]
+        pltpu.make_async_copy(part, part, send_sem).wait()
+        out_part = o_ref.at[pl.ds(0, (pieces - 1) * ROWS)]
+        pltpu.make_async_copy(out_part, out_part, out_recv_sem).wait()
+        pltpu.make_async_copy(recv, recv, out_send_sem).wait()
+
+    @pl.when(mine >= pieces)
+    def _():
+        pltpu.make_async_copy(x_ref, x_ref, send_sem).wait()
+        pltpu.make_async_copy(o_ref, o_ref, out_recv_sem).wait()
+
+
+def all_sum(partials):
+    total = lax.axis_size("lat") * lax.axis_size("lon")
+    shapes = [p.shape for p in partials]
+    flat = jnp.concatenate([p.astype(jnp.bfloat16).reshape(-1, 128) for p in partials], axis=0)
+    used = flat.shape[0]
+    pieces = -(-used // ROWS)
+    flat = jnp.pad(flat, ((0, pieces * ROWS - used), (0, 0)))
+    summed = pl.pallas_call(
+        functools.partial(all_sum_kernel, pieces, pow(STRIDE, -1, total)),
+        out_shape=jax.ShapeDtypeStruct(flat.shape, flat.dtype),
+        in_specs=[pl.BlockSpec(memory_space=pltpu.VMEM)],
+        out_specs=pl.BlockSpec(memory_space=pltpu.VMEM),
+        scratch_shapes=[
+            pltpu.VMEM((ROWS, 128), jnp.bfloat16),
+            pltpu.VMEM(((total - 1) * ROWS, 128), jnp.bfloat16),
+        ]
+        + [pltpu.SemaphoreType.DMA(())] * 4,
+        compiler_params=pltpu.CompilerParams(
+            collective_id=0, has_side_effects=True, vmem_limit_bytes=16 << 20
+        ),
+    )(flat)
+    outs = []
+    start = 0
+    for shape in shapes:
+        count = 1
+        for size in shape:
+            count *= size
+        rows = count // 128
+        outs.append(summed[start : start + rows].astype(jnp.float32).reshape(shape))
+        start += rows
+    return outs
 
 
 def shards(
@@ -219,9 +338,7 @@
         window_embed.astype(jnp.float32).T, g_window, precision=lax.Precision.HIGHEST
     )
     partials = (grad_projection, grad_kernel, grad_gain, grad_in, grad_out)
-    totals = lax.psum(
-        (partials[0], partials[1], partials[2], partials[3], partials[4]), ("lat", "lon")
-    )
+    totals = all_sum(partials)
     return (grad_state, grad_embed, totals[0], totals[1], totals[2], totals[3], totals[4])
 
 

time: 304 us -> 168 us (0.55)
  the two profiles are of different devices: /device:TPU:1 before, /device:TPU:16 now
where the time goes in v1:
time: 168 us; the launch traced here: 167 us
  matrix products  48.1 us (29%)
  other arithmetic  35.9 us (21%)
  starting transfers between devices  30.1 us (18%)
  Pallas kernels  25.6 us (15%)
  waiting for transfers between devices  16.6 us (10%)
  local copies, waits for them, and re-layouts  8.32 us (5%)
  between operations  2.43 us (1%)
    pallas_call x1, Pallas kernels, all_sum(): pl.pallas_call(functools.partial(all_sum_kernel, pieces, pow(STRIDE, -1,...  25.6 us
    dot_general x3, matrix products, backward_block(): lax.dot_general(dense, triple[2], (((0,), (0,)), ((), ())), precision=lax...  19.6 us
    dot_general x3, matrix products, forward_block(): return jnp.dot(dense, window, precision=lax.Precision.HIGHEST)  17.5 us
    ppermute x4, starting transfers between devices, with_halo(): lax.ppermute(lax.slice_in_dim(block, 0, width, axis=dim), axis, backward)  16.5 us
    ppermute x2, waiting for transfers between devices, shifted(): return lax.ppermute(x, axis, pairs)  8.9 us
    reduce_sum x3, other arithmetic, kernel_grad(): jnp.sum(grad * padded[row_tap:row_tap + height, col_tap:col_tap + width],...  8.66 us
    reduce_sum x1, other arithmetic, norm_forward(): center = field - jnp.mean(field, axis=-1, keepdims=True)  8.41 us
    add x1, other arithmetic, shards(): grad_state = g_out + depthwise_back(g_padded, dw_kernel)  8.26 us
  transfers between devices with their start and end apart: 10, of which 5 were waited for; matrix products, arithmetic and copies ran while one was open for 5% of the time, Pallas kernels for 0%

profile of v1, /device:TPU:16, one launch (start us, length us, event | category | flops | bytes accessed | tf_op | source)
XLA Modules:
  0.0 167.2 jit_solution(4612939548160352074)
XLA Ops:
  0.6 4.0 %collective-permute-start = (bf16[512,256]{1,0:T(8,128)(2,1)}, bf16[512,256]{1,0:T(8,128)(2,1)S(1)}, u32[]{:S(2)}, u32[]{:S(2)}) collective-permute-start(bf16[512,256]{1,0:T(8,128)(2,1)} %param.17), channel_id=1, source_target_pairs={{8,0},{16,8},{24,16},{32,24},{40,32},{48,40},{56,48},{64,56},{72,6... | collective-permute-start | bytes 786440 | tf_op jit(solution)/shard_map/ppermute | solution.py:15
  4.7 1.0 constant_dynamic-update-slice_fusion.1
  5.7 1.0 slice_bitcast_fusion.48
  6.7 2.2 %collective-permute-done = bf16[512,256]{1,0:T(8,128)(2,1)S(1)} collective-permute-done((bf16[512,256]{1,0:T(8,128)(2,1)}, bf16[512,256]{1,0:T(8,128)(2,1)S(1)}, u32[]{:S(2)}, u32[]{:S(2)}) %collective-permute-start) | collective-permute-done | bytes 262176 | tf_op jit(solution)/shard_map/ppermute | solution.py:15
  8.9 1.2 convolution_convert_fusion
  10.2 17.9 %while.21 = (s32[]{:T(128)}, f32[3,768,128]{2,1,0:T(8,128)S(1)}, s32[3,4,768]{2,1,0:T(4,128)S(1)}, f32[3,4,768]{2,1,0:T(4,128)S(1)}, f32[1024,128]{1,0:T(8,128)S...) while((s32[]{:T(128)}, f32[3,768,128]{2,1,0:T(8,128)S(1)}, s32[3,4,768]{2,1,0:T(4,128)S(1)}, ...), condition=%wide.region_1.2_spmd, body=%wide.region_0.1_spmd.sunk | while | flops 1216610304 | bytes 999605 | solution.py:293
  10.3 5.8 %fusion.139 = f32[3,768,128]{2,1,0:T(8,128)S(1)} fusion(f32[3,768,128]{2,1,0:T(8,128)S(1)} %get-tuple-element.338, s32[]{:T(128)S(6)} %copy.22, f32[1024,128]{1,0:T(8,128)S(1)} %get-tuple-element.351, f32[768]{0:T(1024)S(1)} %get-tuple-element.306, s32[768]{0:T(1024)S(1)} %get-tuple-element.307, f32[768]{0:T(1024)S(1)} %get-tuple-element.308, ...), kind=kOutput, calls=%fused_computation.22.clone.1 | convolution fusion | flops 1216610304 | bytes 950276 | tf_op jit(solution)/shard_map/while/body/eval_jaxpr/dot_general | solution.py:291
  16.2 5.8 %fusion.139 = f32[3,768,128]{2,1,0:T(8,128)S(1)} fusion(f32[3,768,128]{2,1,0:T(8,128)S(1)} %get-tuple-element.338, s32[]{:T(128)S(6)} %copy.22, f32[1024,128]{1,0:T(8,128)S(1)} %get-tuple-element.351, f32[768]{0:T(1024)S(1)} %get-tuple-element.306, s32[768]{0:T(1024)S(1)} %get-tuple-element.307, f32[768]{0:T(1024)S(1)} %get-tuple-element.308, ...), kind=kOutput, calls=%fused_computation.22.clone.1 | convolution fusion | flops 1216610304 | bytes 950276 | tf_op jit(solution)/shard_map/while/body/eval_jaxpr/dot_general | solution.py:291
  22.2 5.8 %fusion.139 = f32[3,768,128]{2,1,0:T(8,128)S(1)} fusion(f32[3,768,128]{2,1,0:T(8,128)S(1)} %get-tuple-element.338, s32[]{:T(128)S(6)} %copy.22, f32[1024,128]{1,0:T(8,128)S(1)} %get-tuple-element.351, f32[768]{0:T(1024)S(1)} %get-tuple-element.306, s32[768]{0:T(1024)S(1)} %get-tuple-element.307, f32[768]{0:T(1024)S(1)} %get-tuple-element.308, ...), kind=kOutput, calls=%fused_computation.22.clone.1 | convolution fusion | flops 1216610304 | bytes 950276 | tf_op jit(solution)/shard_map/while/body/eval_jaxpr/dot_general | solution.py:291
  28.0 1.2 convert_add_fusion.1
  29.3 2.3 %collective-permute-start.1 = (f32[9,3,128]{2,1,0:T(4,128)S(1)}, f32[9,3,128]{2,1,0:T(4,128)S(1)}, u32[]{:S(2)}, u32[]{:S(2)}) collective-permute-start(f32[9,3,128]{2,1,0:T(4,128)S(1)} %get-tuple-element.174), channel_id=1, source_target_pairs={{0,1},{1,2},{2,3},{3,4},{4,5},{5,6},{6,7},{7,0},{8,9},{9,10},{10,1... | collective-permute-start | bytes 41480 | tf_op jit(solution)/shard_map/ppermute | solution.py:24
  31.6 3.5 %collective-permute-start.2 = (f32[9,3,128]{2,1,0:T(4,128)S(1)}, f32[9,3,128]{2,1,0:T(4,128)S(1)}, u32[]{:S(2)}, u32[]{:S(2)}) collective-permute-start(f32[9,3,128]{2,1,0:T(4,128)S(1)} %get-tuple-element.175), channel_id=1, source_target_pairs={{1,0},{2,1},{3,2},{4,3},{5,4},{6,5},{7,6},{0,7},{9,8},{10,9},{11,1... | collective-permute-start | bytes 41480 | tf_op jit(solution)/shard_map/ppermute | solution.py:27
  35.1 0.6 slice_bitcast_fusion.47
  35.8 1.0 collective-permute-done.1
  36.9 5.3 %collective-permute-start.4 = (f32[3,262,128]{2,1,0:T(8,128)S(1)}, f32[3,262,128]{2,1,0:T(8,128)}, u32[]{:S(2)}, u32[]{:S(2)}) collective-permute-start(f32[3,262,128]{2,1,0:T(8,128)S(1)} %get-tuple-element.172), channel_id=1, source_target_pairs={{8,0},{16,8},{24,16},{32,24},{40,32},{48,40},{56,48},{64,56},{72,6... | collective-permute-start | bytes 1207304 | tf_op jit(solution)/shard_map/ppermute | solution.py:27
  42.3 0.6 slice_bitcast_fusion.46
  43.6 4.3 %collective-permute-done.3 = f32[3,262,128]{2,1,0:T(8,128)S(1)} collective-permute-done((f32[3,262,128]{2,1,0:T(8,128)S(1)}, f32[3,262,128]{2,1,0:T(8,128)S(1)}, u32[]{:S(2)}, u32[]{:S(2)}) %collective-permute-start.3) | collective-permute-done | bytes 402464 | tf_op jit(solution)/shard_map/ppermute | solution.py:24
  47.8 0.7 copy-done.17
  48.6 1.3 maximum_multiply_fusion
  50.2 8.4 %fusion.110 = (f32[9,256]{1,0:T(8,128)S(1)}, f32[9,256,128]{2,1,0:T(8,128)S(1)}) fusion(f32[128]{0:T(128)S(1)} %copy-done.78, f32[15,262,128]{2,1,0:T(8,128)S(1)} %maximum_multiply_fusion, f32[128]{0:T(128)S(1)} %copy-done.80, f32[128]{0:T(128)S(1)} %get-tuple-element.183, f32[128]{0:T(128)S(1)} %get-tuple-element.184, f32[128]{0:T(128)S(1)} %get-tuple-element.185, ...), kind=kLoop, calls=%fused_computation.364 | loop fusion | flops 28899072 | bytes 59016704 | tf_op jit(solution)/shard_map/reduce_sum | solution.py:76
  58.7 0.7 multiply_reduce_fusion.52
  59.4 0.8 multiply_convert_fusion.2
  60.3 0.7 fusion.113
  61.3 3.5 %fusion.54 = bf16[2304,512]{1,0:T(8,128)(2,1)S(1)} fusion(f32[2304,512]{1,0:T(8,128)S(1)} %fusion.113, bf16[2304,128]{1,0:T(8,128)(2,1)S(1)} %bitcast.300, bf16[512,128]{1,0:T(8,128)(2,1)S(1)} %copy-done.100), kind=kOutput, calls=%fused_computation.74 | convolution fusion | flops 325582848 | bytes 7798784 | tf_op jit(solution)/shard_map/dot_general | solution.py:103
  64.8 1.8 %multiply_reduce_fusion.51 = (f32[2304]{0:T(1024)S(1)}, f32[2304,128]{1,0:T(8,128)}) fusion(f32[128]{0:T(128)S(1)} %copy-done.21, bf16[2304,512]{1,0:T(8,128)(2,1)S(1)} %fusion.54, bf16[128,512]{1,0:T(8,128)(2,1)S(1)} %copy-done), kind=kOutput, calls=%fused_computation.232 | convolution fusion | flops 302577408 | bytes 3679744 | tf_op jit(solution)/shard_map/dot_general | solution.py:110
  66.6 2.9 %multiply_reduce_fusion = (bf16[128]{0:T(256)(128)(2,1)}, f32[9,256]{1,0:T(8,128)S(1)}) fusion(f32[9,256,128]{2,1,0:T(8,128)} %bitcast.291, f32[9,256]{1,0:T(8,128)S(1)} %add_sqrt_fusion, f32[9,256,128]{2,1,0:T(8,128)S(1)} %get-tuple-element.170, f32[9,256]{1,0:T(8,128)S(1)} %broadcast_multiply_fusion.1, f32[128]{0:T(128)S(1)} %copy-done.21), kind=kLoop, calls=%fused_computation.180 | loop fusion | flops 2061952 | bytes 2387712 | tf_op jit(solution)/shard_map/reduce_sum | solution.py:82
  69.5 4.1 %multiply_reduce_fusion.1 = (bf16[128]{0:T(256)(128)(2,1)S(1)}, bf16[128]{0:T(256)(128)(2,1)S(1)}, bf16[128]{0:T(256)(128)(2,1)S(1)}, bf16[128]{0:T(256)(128)(2,...) fusion(f32[15,262,128]{2,1,0:T(8,128)S(1)} %maximum_multiply_fu, ...), kind=kLoop, calls=%fused_computation.181 | loop fusion | flops 12678912 | bytes 24814592 | tf_op jit(solution)/shard_map/reduce_sum | solution.py:67
  73.6 1.9 %multiply_reduce_fusion.37 = (bf16[128]{0:T(256)(128)(2,1)S(1)}, bf16[128]{0:T(256)(128)(2,1)S(1)}, bf16[128]{0:T(256)(128)(2,1)S(1)}, bf16[128]{0:T(256)(128)(2...) fusion(f32[9,256,128]{2,1,0:T(8,128)S(1)} %get-tuple-element.16, ...), kind=kLoop, calls=%fused_computation.217 | loop fusion | flops 7666048 | bytes 16518400 | tf_op jit(solution)/shard_map/reduce_sum | solution.py:67
  75.5 2.7 %multiply_reduce_fusion.19 = (bf16[128]{0:T(256)(128)(2,1)S(1)}, bf16[128]{0:T(256)(128)(2,1)S(1)}, bf16[128]{0:T(256)(128)(2,1)S(1)}, bf16[128]{0:T(256)(128)(2...) fusion(f32[9,256,128]{2,1,0:T(8,128)S(1)} %get-tuple-element.16, ...), kind=kLoop, calls=%fused_computation.199 | loop fusion | flops 10909440 | bytes 23007744 | tf_op jit(solution)/shard_map/reduce_sum | solution.py:67
  78.2 5.0 %collective-permute-start.5 = (bf16[9,3,128]{2,1,0:T(4,128)(2,1)S(1)}, bf16[9,3,128]{2,1,0:T(4,128)(2,1)S(1)}, u32[]{:S(2)}, u32[]{:S(2)}) collective-permute-start(bf16[9,3,128]{2,1,0:T(4,128)(2,1)S(1)} %get-tuple-element.178), channel_id=1, source_target_pairs={{0,1},{1,2},{2,3},{3,4},{4,5},{5,6},{6,7},{7,0},{8,9},{9,10},{10,1... | collective-permute-start | bytes 20744 | tf_op jit(solution)/shard_map/ppermute | solution.py:24
  83.2 2.3 %collective-permute-start.6 = (bf16[9,3,128]{2,1,0:T(4,128)(2,1)S(1)}, bf16[9,3,128]{2,1,0:T(4,128)(2,1)S(1)}, u32[]{:S(2)}, u32[]{:S(2)}) collective-permute-start(bf16[9,3,128]{2,1,0:T(4,128)(2,1)S(1)} %get-tuple-element.179), channel_id=1, source_target_pairs={{1,0},{2,1},{3,2},{4,3},{5,4},{6,5},{7,6},{0,7},{9,8},{10,9},{11,1... | collective-permute-start | bytes 20744 | tf_op jit(solution)/shard_map/ppermute | solution.py:27
  85.6 2.0 %fusion.105 = bf16[512,128]{1,0:T(8,128)(2,1)S(1)} fusion(bf16[2304,128]{1,0:T(8,128)(2,1)S(1)} %bitcast.301, f32[2304,512]{1,0:T(8,128)S(1)} %bitcast.296), kind=kOutput, calls=%fused_computation.237 | convolution fusion | flops 312672256 | bytes 5439488 | tf_op jit(solution)/shard_map/dot_general | solution.py:100
  87.8 5.3 %collective-permute-start.8 = (bf16[3,262,128]{2,1,0:T(8,128)(2,1)S(1)}, bf16[3,262,128]{2,1,0:T(8,128)(2,1)S(1)}, u32[]{:S(2)}, u32[]{:S(2)}) collective-permute-start(bf16[3,262,128]{2,1,0:T(8,128)(2,1)S(1)} %get-tuple-element.177), channel_id=1, source_target_pairs={{8,0},{16,8},{24,16},{32,24},{40,32},{48,40},{56,48},{64,56},{72,6... | collective-permute-start | bytes 603656 | tf_op jit(solution)/shard_map/ppermute | solution.py:27
  94.1 2.5 %collective-permute-done.7 = bf16[3,262,128]{2,1,0:T(8,128)(2,1)S(1)} collective-permute-done((bf16[3,262,128]{2,1,0:T(8,128)(2,1)S(1)}, bf16[3,262,128]{2,1,0:T(8,128)(2,1)S(1)}, u32[]{:S(2)}, u32[]{:S(2)}) %collective-permute-start.7) | collective-permute-done | bytes 201248 | tf_op jit(solution)/shard_map/ppermute | solution.py:24
  97.1 8.3 %convert_add_fusion = f32[9,256,128]{2,1,0:T(8,128)S(1)} fusion(bf16[9,256,128]{2,1,0:T(8,128)(2,1)S(1)} %copy-done.10, f32[15,262,128]{2,1,0:T(8,128)S(1)} %convert_multiply_fusion, f32[128]{0:T(128)S(1)} %copy-done.79, f32[128]{0:T(128)S(1)} %copy-done.81, f32[128]{0:T(128)S(1)} %get-tuple-element.183, f32[128]{0:T(128)S(1)} %get-tuple-element.184, ...), kind=kLoop, calls=%fused_computation.79 | loop fusion | flops 29196288 | bytes 59597312 | tf_op jit(solution)/shard_map/add | solution.py:311
  105.4 20.0 %while.22 = (s32[]{:T(128)}, f32[1024,128]{1,0:T(8,128)S(1)}, s32[3,4,768]{2,1,0:T(4,128)S(1)}, f32[3,4,768]{2,1,0:T(4,128)S(1)}, f32[3,768,128]{2,1,0:T(8,128)S...) while((s32[]{:T(128)}, f32[1024,128]{1,0:T(8,128)S(1)}, s32[3,4,768]{2,1,0:T(4,128)S(1)}, ...), condition=%wide.region_7.8_spmd.clone, body=%wide.region_6.7_spmd.clone.sunk | while | flops 1216872448 | bytes 1523903 | solution.py:325
  105.6 6.5 %fusion.142 = f32[1024,128]{1,0:T(8,128)S(1)} fusion(f32[768]{0:T(1024)S(1)} %get-tuple-element.319, s32[768]{0:T(1024)S(1)} %get-tuple-element.320, f32[768]{0:T(1024)S(1)} %get-tuple-element.321, s32[768]{0:T(1024)S(1)} %get-tuple-element.322, f32[768]{0:T(1024)S(1)} %get-tuple-element.323, s32[768]{0:T(1024)S(1)} %get-tuple-element.324, ...), kind=kOutput, calls=%fused_computation.53.clone.1 | convolution fusion | flops 1216872448 | bytes 1474565 | tf_op jit(solution)/shard_map/while/body/eval_jaxpr/dot_general | solution.py:316
  112.2 6.5 %fusion.142 = f32[1024,128]{1,0:T(8,128)S(1)} fusion(f32[768]{0:T(1024)S(1)} %get-tuple-element.319, s32[768]{0:T(1024)S(1)} %get-tuple-element.320, f32[768]{0:T(1024)S(1)} %get-tuple-element.321, s32[768]{0:T(1024)S(1)} %get-tuple-element.322, f32[768]{0:T(1024)S(1)} %get-tuple-element.323, s32[768]{0:T(1024)S(1)} %get-tuple-element.324, ...), kind=kOutput, calls=%fused_computation.53.clone.1 | convolution fusion | flops 1216872448 | bytes 1474565 | tf_op jit(solution)/shard_map/while/body/eval_jaxpr/dot_general | solution.py:316
  118.9 6.5 %fusion.142 = f32[1024,128]{1,0:T(8,128)S(1)} fusion(f32[768]{0:T(1024)S(1)} %get-tuple-element.319, s32[768]{0:T(1024)S(1)} %get-tuple-element.320, f32[768]{0:T(1024)S(1)} %get-tuple-element.321, s32[768]{0:T(1024)S(1)} %get-tuple-element.322, f32[768]{0:T(1024)S(1)} %get-tuple-element.323, s32[768]{0:T(1024)S(1)} %get-tuple-element.324, ...), kind=kOutput, calls=%fused_computation.53.clone.1 | convolution fusion | flops 1216872448 | bytes 1474565 | tf_op jit(solution)/shard_map/while/body/eval_jaxpr/dot_general | solution.py:316
  125.7 0.7 convolution_convert_fusion.2
  126.5 1.5 concatenate.24
  128.1 25.6 %shard_map.162 = bf16[1344,128]{1,0:T(8,128)(2,1)S(1)} custom-call(bf16[1344,128]{1,0:T(8,128)(2,1)S(1)} %pad.4.x_ref), custom_call_target="tpu_custom_call" | custom-call | tf_op jit(solution)/shard_map/pallas_call | solution.py:233
  153.7 0.8 slice_convert_fusion.1
  155.1 2.1 %collective-permute-start.9 = (bf16[512,256]{1,0:T(8,128)(2,1)S(1)}, bf16[512,256]{1,0:T(8,128)(2,1)S(1)}, u32[]{:S(2)}, u32[]{:S(2)}) collective-permute-start(bf16[512,256]{1,0:T(8,128)(2,1)S(1)} %slice.1320), channel_id=1, source_target_pairs={{0,8},{8,16},{16,24},{24,32},{32,40},{40,48},{48,56},{56,64},{64,7... | collective-permute-start | bytes 786440 | tf_op jit(solution)/shard_map/ppermute | solution.py:15
  158.3 0.7 reshape.172
  159.0 0.7 slice_convert_fusion.3
  159.7 6.7 %collective-permute-done.9 = bf16[512,256]{1,0:T(8,128)(2,1)S(1)} collective-permute-done((bf16[512,256]{1,0:T(8,128)(2,1)S(1)}, bf16[512,256]{1,0:T(8,128)(2,1)S(1)}, u32[]{:S(2)}, u32[]{:S(2)}) %collective-permute-start.9) | collective-permute-done | bytes 262176 | tf_op jit(solution)/shard_map/ppermute | solution.py:15
  166.4 0.8 slice_add_fusion
  (250 shorter events, 4.8 us)
Async XLA Ops:
  0.6 59.6 %copy-start = (bf16[128,512]{1,0:T(8,128)(2,1)S(1)}, bf16[128,512]{1,0:T(8,128)(2,1)}, u32[]{:S(2)}) copy-start(bf16[128,512]{1,0:T(8,128)(2,1)} %param.21) | copy-start | bytes 393220
  0.6 8.2 %collective-permute-start = (bf16[512,256]{1,0:T(8,128)(2,1)}, bf16[512,256]{1,0:T(8,128)(2,1)S(1)}, u32[]{:S(2)}, u32[]{:S(2)}) collective-permute-start(bf16[512,256]{1,0:T(8,128)(2,1)} %param.17), channel_id=1, source_target_pairs={{8,0},{16,8},{24,16},{32,24},{40,32},{48,40},{56,48},{64,56},{72,6... | collective-permute-start | bytes 786440 | tf_op jit(solution)/shard_map/ppermute | solution.py:15
  28.0 7.1 %copy-start.19 = (f32[7,7,128]{2,1,0:T(8,128)S(1)}, f32[7,7,128]{2,1,0:T(8,128)}, u32[]{:S(2)}) copy-start(f32[7,7,128]{2,1,0:T(8,128)} %param.19) | copy-start | bytes 75268
  29.3 13.6 %copy-start.20 = (s32[9,256]{1,0:T(8,128)S(1)}, s32[9,256]{1,0:T(8,128)}, u32[]{:S(2)}) copy-start(s32[9,256]{1,0:T(8,128)} %param.25) | copy-start | bytes 27652
  29.3 13.7 %copy-start.9 = (bf16[9,256,128]{2,1,0:T(8,128)(2,1)S(1)}, bf16[9,256,128]{2,1,0:T(8,128)(2,1)}, u32[]{:S(2)}) copy-start(bf16[9,256,128]{2,1,0:T(8,128)(2,1)} %param.16) | copy-start | bytes 1769476
  29.3 7.5 %collective-permute-start.1 = (f32[9,3,128]{2,1,0:T(4,128)S(1)}, f32[9,3,128]{2,1,0:T(4,128)S(1)}, u32[]{:S(2)}, u32[]{:S(2)}) collective-permute-start(f32[9,3,128]{2,1,0:T(4,128)S(1)} %get-tuple-element.174), channel_id=1, source_target_pairs={{0,1},{1,2},{2,3},{3,4},{4,5},{5,6},{6,7},{7,0},{8,9},{9,10},{10,1... | collective-permute-start | bytes 41480 | tf_op jit(solution)/shard_map/ppermute | solution.py:24
  31.6 5.2 %collective-permute-start.2 = (f32[9,3,128]{2,1,0:T(4,128)S(1)}, f32[9,3,128]{2,1,0:T(4,128)S(1)}, u32[]{:S(2)}, u32[]{:S(2)}) collective-permute-start(f32[9,3,128]{2,1,0:T(4,128)S(1)} %get-tuple-element.175), channel_id=1, source_target_pairs={{1,0},{2,1},{3,2},{4,3},{5,4},{6,5},{7,6},{0,7},{9,8},{10,9},{11,1... | collective-permute-start | bytes 41480 | tf_op jit(solution)/shard_map/ppermute | solution.py:27
  35.7 14.2 %copy-start.22 = (f32[128]{0:T(128)}, f32[128]{0:T(128)S(1)}, u32[]{:S(2)}) copy-start(f32[128]{0:T(128)S(1)} %get-tuple-element.201) | copy-start | bytes 1540
  35.8 14.2 %copy-start.24 = (f32[128]{0:T(128)}, f32[128]{0:T(128)S(1)}, u32[]{:S(2)}) copy-start(f32[128]{0:T(128)S(1)} %get-tuple-element.202) | copy-start | bytes 1540
  35.8 14.2 %copy-start.26 = (f32[128]{0:T(128)}, f32[128]{0:T(128)S(1)}, u32[]{:S(2)}) copy-start(f32[128]{0:T(128)S(1)} %get-tuple-element.203) | copy-start | bytes 1540
  35.8 14.2 %copy-start.28 = (f32[128]{0:T(128)}, f32[128]{0:T(128)S(1)}, u32[]{:S(2)}) copy-start(f32[128]{0:T(128)S(1)} %get-tuple-element.204) | copy-start | bytes 1540
  35.8 14.2 %copy-start.30 = (f32[128]{0:T(128)}, f32[128]{0:T(128)S(1)}, u32[]{:S(2)}) copy-start(f32[128]{0:T(128)S(1)} %get-tuple-element.205) | copy-start | bytes 1540
  35.8 14.2 %copy-start.32 = (f32[128]{0:T(128)}, f32[128]{0:T(128)S(1)}, u32[]{:S(2)}) copy-start(f32[128]{0:T(128)S(1)} %get-tuple-element.206) | copy-start | bytes 1540
  36.8 11.0 %collective-permute-start.3 = (f32[3,262,128]{2,1,0:T(8,128)S(1)}, f32[3,262,128]{2,1,0:T(8,128)S(1)}, u32[]{:S(2)}, u32[]{:S(2)}) collective-permute-start(f32[3,262,128]{2,1,0:T(8,128)S(1)} %get-tuple-element.171), channel_id=1, source_target_pairs={{0,8},{8,16},{16,24},{24,32},{32,40},{40,48},{48,56},{56,64},{64,7... | collective-permute-start | bytes 1207304 | tf_op jit(solution)/shard_map/ppermute | solution.py:24
  36.9 11.7 %collective-permute-start.4 = (f32[3,262,128]{2,1,0:T(8,128)S(1)}, f32[3,262,128]{2,1,0:T(8,128)}, u32[]{:S(2)}, u32[]{:S(2)}) collective-permute-start(f32[3,262,128]{2,1,0:T(8,128)S(1)} %get-tuple-element.172), channel_id=1, source_target_pairs={{8,0},{16,8},{24,16},{32,24},{40,32},{48,40},{56,48},{64,56},{72,6... | collective-permute-start | bytes 1207304 | tf_op jit(solution)/shard_map/ppermute | solution.py:27
  42.9 7.0 %copy-start.97 = (f32[15]{0:T(128)}, f32[15]{0:T(128)S(1)}, u32[]{:S(2)}) copy-start(f32[15]{0:T(128)S(1)} %or_select_fusion) | copy-start | bytes 184
  43.3 17.7 %copy-start.13 = (bf16[9,256,128]{2,1,0:T(8,128)(2,1)}, bf16[9,256,128]{2,1,0:T(8,128)(2,1)S(1)}, u32[]{:S(2)}) copy-start(bf16[9,256,128]{2,1,0:T(8,128)(2,1)S(1)} %fusion.56) | copy-start | bytes 1769476
  43.3 6.7 %copy-start.34 = (f32[128]{0:T(128)S(1)}, f32[128]{0:T(128)}, u32[]{:S(2)}) copy-start(f32[128]{0:T(128)} %get-tuple-element.207) | copy-start | bytes 1540
  43.3 6.7 %copy-start.36 = (f32[128]{0:T(128)S(1)}, f32[128]{0:T(128)}, u32[]{:S(2)}) copy-start(f32[128]{0:T(128)} %get-tuple-element.208) | copy-start | bytes 1540
  43.3 6.7 %copy-start.38 = (f32[128]{0:T(128)S(1)}, f32[128]{0:T(128)}, u32[]{:S(2)}) copy-start(f32[128]{0:T(128)} %get-tuple-element.209) | copy-start | bytes 1540
  43.4 6.7 %copy-start.40 = (f32[128]{0:T(128)S(1)}, f32[128]{0:T(128)}, u32[]{:S(2)}) copy-start(f32[128]{0:T(128)} %get-tuple-element.210) | copy-start | bytes 1540
  43.4 6.7 %copy-start.42 = (f32[128]{0:T(128)S(1)}, f32[128]{0:T(128)}, u32[]{:S(2)}) copy-start(f32[128]{0:T(128)} %get-tuple-element.211) | copy-start | bytes 1540
  43.4 6.7 %copy-start.44 = (f32[128]{0:T(128)S(1)}, f32[128]{0:T(128)}, u32[]{:S(2)}) copy-start(f32[128]{0:T(128)} %get-tuple-element.212) | copy-start | bytes 1540
  43.4 6.7 %copy-start.46 = (f32[128]{0:T(128)S(1)}, f32[128]{0:T(128)}, u32[]{:S(2)}) copy-start(f32[128]{0:T(128)} %get-tuple-element.213) | copy-start | bytes 1540
  43.4 6.7 %copy-start.48 = (f32[128]{0:T(128)S(1)}, f32[128]{0:T(128)}, u32[]{:S(2)}) copy-start(f32[128]{0:T(128)} %get-tuple-element.214) | copy-start | bytes 1540
  43.4 6.7 %copy-start.50 = (f32[128]{0:T(128)S(1)}, f32[128]{0:T(128)}, u32[]{:S(2)}) copy-start(f32[128]{0:T(128)} %get-tuple-element.215) | copy-start | bytes 1540
  43.4 6.7 %copy-start.52 = (f32[128]{0:T(128)S(1)}, f32[128]{0:T(128)}, u32[]{:S(2)}) copy-start(f32[128]{0:T(128)} %get-tuple-element.216) | copy-start | bytes 1540
  43.4 6.7 %copy-start.54 = (f32[128]{0:T(128)S(1)}, f32[128]{0:T(128)}, u32[]{:S(2)}) copy-start(f32[128]{0:T(128)} %get-tuple-element.217) | copy-start | bytes 1540
  43.4 6.7 %copy-start.56 = (f32[128]{0:T(128)S(1)}, f32[128]{0:T(128)}, u32[]{:S(2)}) copy-start(f32[128]{0:T(128)} %get-tuple-element.218) | copy-start | bytes 1540
  43.4 6.7 %copy-start.58 = (f32[128]{0:T(128)S(1)}, f32[128]{0:T(128)}, u32[]{:S(2)}) copy-start(f32[128]{0:T(128)} %get-tuple-element.219) | copy-start | bytes 1540
  43.5 6.7 %copy-start.60 = (f32[128]{0:T(128)S(1)}, f32[128]{0:T(128)}, u32[]{:S(2)}) copy-start(f32[128]{0:T(128)} %get-tuple-element.220) | copy-start | bytes 1540
  43.5 6.7 %copy-start.62 = (f32[128]{0:T(128)S(1)}, f32[128]{0:T(128)}, u32[]{:S(2)}) copy-start(f32[128]{0:T(128)} %get-tuple-element.221) | copy-start | bytes 1540
  43.5 6.7 %copy-start.64 = (f32[128]{0:T(128)S(1)}, f32[128]{0:T(128)}, u32[]{:S(2)}) copy-start(f32[128]{0:T(128)} %get-tuple-element.222) | copy-start | bytes 1540
  43.5 6.7 %copy-start.66 = (f32[128]{0:T(128)S(1)}, f32[128]{0:T(128)}, u32[]{:S(2)}) copy-start(f32[128]{0:T(128)} %get-tuple-element.223) | copy-start | bytes 1540
  43.5 6.7 %copy-start.68 = (f32[128]{0:T(128)S(1)}, f32[128]{0:T(128)}, u32[]{:S(2)}) copy-start(f32[128]{0:T(128)} %get-tuple-element.224) | copy-start | bytes 1540
  73.6 12.0 %slice-start = ((s8[4718592]{0:T(1024)(128)(4,1)}), s8[4194304]{0:T(1024)(128)(4,1)S(1)}, s32[]{:S(2)}) async-start(s8[4718592]{0:T(1024)(128)(4,1)} %bitcast.295), calls=%async_computation | async-start | bytes 8388608
  75.5 10.1 %slice-start.1 = ((s8[4718592]{0:T(1024)(128)(4,1)}), s8[524288]{0:T(1024)(128)(4,1)S(1)}, s32[]{:S(2)}) async-start(s8[4718592]{0:T(1024)(128)(4,1)} %bitcast.295), calls=%async_computation.1 | async-start | bytes 1048576
  75.5 10.1 %copy-start.14 = (bf16[9,256,128]{2,1,0:T(8,128)(2,1)S(1)}, bf16[9,256,128]{2,1,0:T(8,128)(2,1)}, u32[]{:S(2)}) copy-start(bf16[9,256,128]{2,1,0:T(8,128)(2,1)} %copy-done.13) | copy-start | bytes 1769476
  78.2 9.4 %collective-permute-start.5 = (bf16[9,3,128]{2,1,0:T(4,128)(2,1)S(1)}, bf16[9,3,128]{2,1,0:T(4,128)(2,1)S(1)}, u32[]{:S(2)}, u32[]{:S(2)}) collective-permute-start(bf16[9,3,128]{2,1,0:T(4,128)(2,1)S(1)} %get-tuple-element.178), channel_id=1, source_target_pairs={{0,1},{1,2},{2,3},{3,4},{4,5},{5,6},{6,7},{7,0},{8,9},{9,10},{10,1... | collective-permute-start | bytes 20744 | tf_op jit(solution)/shard_map/ppermute | solution.py:24
  83.2 4.3 %collective-permute-start.6 = (bf16[9,3,128]{2,1,0:T(4,128)(2,1)S(1)}, bf16[9,3,128]{2,1,0:T(4,128)(2,1)S(1)}, u32[]{:S(2)}, u32[]{:S(2)}) collective-permute-start(bf16[9,3,128]{2,1,0:T(4,128)(2,1)S(1)} %get-tuple-element.179), channel_id=1, source_target_pairs={{1,0},{2,1},{3,2},{4,3},{5,4},{6,5},{7,6},{0,7},{9,8},{10,9},{11,1... | collective-permute-start | bytes 20744 | tf_op jit(solution)/shard_map/ppermute | solution.py:27
  85.6 7.6 %copy-start.3 = (bf16[2304,512]{1,0:T(8,128)(2,1)S(1)}, bf16[2304,512]{1,0:T(8,128)(2,1)}, u32[]{:S(2)}) copy-start(bf16[2304,512]{1,0:T(8,128)(2,1)} %copy-done.2) | copy-start | bytes 7077892
  87.7 8.8 %collective-permute-start.7 = (bf16[3,262,128]{2,1,0:T(8,128)(2,1)S(1)}, bf16[3,262,128]{2,1,0:T(8,128)(2,1)S(1)}, u32[]{:S(2)}, u32[]{:S(2)}) collective-permute-start(bf16[3,262,128]{2,1,0:T(8,128)(2,1)S(1)} %get-tuple-element.176), channel_id=1, source_target_pairs={{0,8},{8,16},{16,24},{24,32},{32,40},{40,48},{48,56},{56,64},{64,7... | collective-permute-start | bytes 603656 | tf_op jit(solution)/shard_map/ppermute | solution.py:24
  87.8 8.8 %copy-start.98 = (f32[15]{0:T(128)S(1)}, f32[15]{0:T(128)}, u32[]{:S(2)}) copy-start(f32[15]{0:T(128)} %copy-done.97) | copy-start | bytes 184
  87.8 8.8 %collective-permute-start.8 = (bf16[3,262,128]{2,1,0:T(8,128)(2,1)S(1)}, bf16[3,262,128]{2,1,0:T(8,128)(2,1)S(1)}, u32[]{:S(2)}, u32[]{:S(2)}) collective-permute-start(bf16[3,262,128]{2,1,0:T(8,128)(2,1)S(1)} %get-tuple-element.177), channel_id=1, source_target_pairs={{8,0},{16,8},{24,16},{32,24},{40,32},{48,40},{56,48},{64,56},{72,6... | collective-permute-start | bytes 603656 | tf_op jit(solution)/shard_map/ppermute | solution.py:27
  97.1 8.3 %copy-start.11 = (f32[1024,128]{1,0:T(8,128)S(1)}, f32[1024,128]{1,0:T(8,128)}, u32[]{:S(2)}) copy-start(f32[1024,128]{1,0:T(8,128)} %custom-call) | copy-start | bytes 1572868
  105.4 20.2 %copy-start.8 = (bf16[1024,256]{1,0:T(8,128)(2,1)S(1)}, bf16[1024,256]{1,0:T(8,128)(2,1)}, u32[]{:S(2)}) copy-start(bf16[1024,256]{1,0:T(8,128)(2,1)} %copy-done.7) | copy-start | bytes 1572868
  128.0 26.4 %copy-start.18 = (bf16[256,128]{1,0:T(8,128)(2,1)S(1)}, bf16[256,128]{1,0:T(8,128)(2,1)}, u32[]{:S(2)}) copy-start(bf16[256,128]{1,0:T(8,128)(2,1)} %param.18) | copy-start | bytes 196612
  155.1 11.3 %collective-permute-start.9 = (bf16[512,256]{1,0:T(8,128)(2,1)S(1)}, bf16[512,256]{1,0:T(8,128)(2,1)S(1)}, u32[]{:S(2)}, u32[]{:S(2)}) collective-permute-start(bf16[512,256]{1,0:T(8,128)(2,1)S(1)} %slice.1320), channel_id=1, source_target_pairs={{0,8},{8,16},{16,24},{24,32},{32,40},{40,48},{48,56},{56,64},{64,7... | collective-permute-start | bytes 786440 | tf_op jit(solution)/shard_map/ppermute | solution.py:15
  (65 other events, 178.6 us)

commit v2 on v0

v2 whole, which is shorter than its diff:
```python
import functools
import jax
import jax.numpy as jnp
from jax import lax
from jax.experimental import pallas as pl
from jax.experimental.pallas import tpu as pltpu
from jax.sharding import PartitionSpec as P

EPSILON = 1e-05
ROWS = 16
STRIDE = 55
EDGE = 8
TAPS = 7
HALF = 3
MESH = pl.DeviceIdType.MESH
VMEM = pltpu.VMEM
LIMIT = 28 << 20


def here():
    lat = lax.axis_index("lat")
    lon = lax.axis_index("lon")
    lats = lax.axis_size("lat")
    lons = lax.axis_size("lon")
    return lat, lon, lats, lons


def halo_copies(pad, top_out, bottom_out, top_in, bottom_in, send_sem, recv_sem):
    lat, lon, lats, lons = here()
    height = pad.shape[0] - 2 * HALF
    width = pad.shape[1] - 2 * EDGE
    left = (lon + lons - 1) % lons
    right = (lon + 1) % lons
    has_up = lat > 0
    has_down = lat < lats - 1
    body = pl.ds(HALF, height)
    first = pl.ds(HALF, HALF)
    last = pl.ds(height, HALF)
    above = pl.ds(0, HALF)
    below = pl.ds(HALF + height, HALF)
    west = pl.ds(EDGE, EDGE)
    east = pl.ds(width, EDGE)
    west_rim = pl.ds(0, EDGE)
    east_rim = pl.ds(EDGE + width, EDGE)
    plan = [
        (top_out, bottom_in, lat - 1, lon, has_up, has_down),
        (bottom_out, top_in, lat + 1, lon, has_down, has_up),
        (pad.at[body, west], pad.at[body, east_rim], lat, left, None, None),
        (pad.at[body, east], pad.at[body, west_rim], lat, right, None, None),
        (pad.at[first, west], pad.at[below, east_rim], lat - 1, left, has_up, has_down),
        (pad.at[first, east], pad.at[below, west_rim], lat - 1, right, has_up, has_down),
        (pad.at[last, west], pad.at[above, east_rim], lat + 1, left, has_down, has_up),
        (pad.at[last, east], pad.at[above, west_rim], lat + 1, right, has_down, has_up),
    ]
    made = []
    for number, (source, target, to_lat, to_lon, sends, receives) in enumerate(plan):
        copy = pltpu.make_async_remote_copy(
            src_ref=source,
            dst_ref=target,
            send_sem=send_sem.at[number],
            recv_sem=recv_sem.at[number],
            device_id={"lat": to_lat, "lon": to_lon},
            device_id_type=MESH,
        )
        made.append((copy, sends, receives))
    return made


def guarded(condition, action):
    if condition is None:
        action()
    else:
        pl.when(condition)(action)


def halo_start(pad, top_out, bottom_out, top_in, bottom_in, send_sem, recv_sem):
    height = pad.shape[0] - 2 * HALF
    width = pad.shape[1] - 2 * EDGE
    inner = pl.ds(EDGE, width)
    top_out[...] = pad[pl.ds(HALF, HALF), inner].astype(jnp.bfloat16)
    bottom_out[...] = pad[pl.ds(height, HALF), inner].astype(jnp.bfloat16)
    copies = halo_copies(pad, top_out, bottom_out, top_in, bottom_in, send_sem, recv_sem)
    for copy, sends, _ in copies:
        guarded(sends, copy.start)


def halo_finish(pad, top_out, bottom_out, top_in, bottom_in, send_sem, recv_sem):
    lat, _, lats, _ = here()
    height = pad.shape[0] - 2 * HALF
    width = pad.shape[1] - 2 * EDGE
    inner = pl.ds(EDGE, width)
    copies = halo_copies(pad, top_out, bottom_out, top_in, bottom_in, send_sem, recv_sem)
    for copy, sends, receives in copies:
        guarded(sends, copy.wait_send)
        guarded(receives, copy.wait_recv)
    blank = jnp.zeros((HALF, pad.shape[1], pad.shape[2]), jnp.float32)

    @pl.when(lat == 0)
    def _():
        pad[pl.ds(0, HALF)] = blank

    @pl.when(lat > 0)
    def _():
        pad[pl.ds(0, HALF), inner] = top_in[...].astype(jnp.float32)

    @pl.when(lat == lats - 1)
    def _():
        pad[pl.ds(HALF + height, HALF)] = blank

    @pl.when(lat < lats - 1)
    def _():
        pad[pl.ds(HALF + height, HALF), inner] = bottom_in[...].astype(jnp.float32)


def forward_kernel(
    embed_ref, proj_ref, index_ref, weight_ref, state_ref, pad, dense,
    own, following, top_out, bottom_out, top_in, bottom_in,
    send_sem, recv_sem, window_send, window_recv,
):
    lat, lon, lats, lons = here()
    margins, height, width = index_ref.shape
    cells = embed_ref.shape[0]
    slots = 2 * cells
    left = (lon + lons - 1) % lons
    right = (lon + 1) % lons
    barrier = pltpu.get_barrier_semaphore()

    def greet(to_lat, to_lon):
        pl.semaphore_signal(
            barrier, inc=1, device_id={"lat": to_lat, "lon": to_lon}, device_id_type=MESH
        )

    greet(lat, left)
    greet(lat, right)

    @pl.when(lat > 0)
    def _():
        for to_lon in (left, lon, right):
            greet(lat - 1, to_lon)

    @pl.when(lat < lats - 1)
    def _():
        for to_lon in (left, lon, right):
            greet(lat + 1, to_lon)

    projected = jnp.dot(embed_ref[...], proj_ref[...], preferred_element_type=jnp.float32)
    own[...] = jnp.transpose(projected).astype(jnp.bfloat16)
    ends = (lat == 0).astype(jnp.int32) + (lat == lats - 1).astype(jnp.int32)
    pl.semaphore_wait(barrier, 8 - 3 * ends)

    window = pltpu.make_async_remote_copy(
        src_ref=own, dst_ref=following, send_sem=window_send, recv_sem=window_recv,
        device_id={"lat": lat - 1, "lon": lon}, device_id_type=MESH,
    )
    pl.when(lat > 0)(window.start)

    step = 32
    base = lax.broadcasted_iota(jnp.int32, (step, width), 0)

    def build(row, carry):
        picks = [index_ref[q, pl.ds(row, 1), :] for q in range(margins)]
        loads = [weight_ref[q, pl.ds(row, 1), :] for q in range(margins)]
        at = pl.ds(pl.multiple_of(row * width, 128), width)
        for start in range(0, slots, step):
            here_slots = base + start
            total = None
            for pick, load in zip(picks, loads):
                term = jnp.where(here_slots == pick, load, 0.0)
                total = term if total is None else total + term
            dense[pl.ds(start, step), at] = total.astype(jnp.bfloat16)
        return carry

    lax.fori_loop(0, height, build, 0)

    @pl.when(lat < lats - 1)
    def _():
        window.wait_recv()

    @pl.when(lat == lats - 1)
    def _():
        following[...] = jnp.zeros(following.shape, jnp.bfloat16)

    pl.when(lat > 0)(window.wait_send)

    def force(row, carry):
        at = pl.ds(pl.multiple_of(row * width, 128), width)
        forcing = jnp.dot(own[...], dense[pl.ds(0, cells), at], preferred_element_type=jnp.float32)
        forcing = forcing + jnp.dot(
            following[...], dense[pl.ds(cells, cells), at], preferred_element_type=jnp.float32
        )
        pad[row + HALF, pl.ds(EDGE, width)] = (
            state_ref[row].astype(jnp.float32) + jnp.transpose(forcing)
        )
        return carry

    lax.fori_loop(0, height, force, 0)
    rims = (pad, top_out, bottom_out, top_in, bottom_in, send_sem, recv_sem)
    halo_start(*rims)
    halo_finish(*rims)


def forward(embed, projection, index, weight, state):
    height, width, channels = state.shape
    slots = 2 * embed.shape[0]
    rim = VMEM((HALF, width, channels), jnp.bfloat16)
    return pl.pallas_call(
        forward_kernel,
        out_shape=(
            jax.ShapeDtypeStruct((height + 2 * HALF, width + 2 * EDGE, channels), jnp.float32),
            jax.ShapeDtypeStruct((slots, height * width), jnp.bfloat16),
        ),
        in_specs=[pl.BlockSpec(memory_space=VMEM)] * 5,
        out_specs=(pl.BlockSpec(memory_space=VMEM),) * 2,
        scratch_shapes=[
            VMEM((channels, embed.shape[0]), jnp.bfloat16),
            VMEM((channels, embed.shape[0]), jnp.bfloat16),
            rim, rim, rim, rim,
            pltpu.SemaphoreType.DMA((8,)),
            pltpu.SemaphoreType.DMA((8,)),
            pltpu.SemaphoreType.DMA(()),
            pltpu.SemaphoreType.DMA(()),
        ],
        compiler_params=pltpu.CompilerParams(
            collective_id=0, has_side_effects=True, vmem_limit_bytes=LIMIT
        ),
    )(embed, projection, index, weight, state)


def depthwise(pad, wide_kernel, out, height, width, flipped):
    def block(column, carry):
        start = pl.multiple_of(column * EDGE, EDGE)
        near = pad.at[:, pl.ds(start, 3 * EDGE), :]
        sums = [None] * height
        for b in range(TAPS):
            offset = EDGE - HALF + b
            rows = [near[r, offset : offset + EDGE, :] for r in range(height + 2 * HALF)]
            for a in range(TAPS):
                tap = (TAPS - 1 - a) * TAPS + TAPS - 1 - b if flipped else a * TAPS + b
                factor = wide_kernel[tap]
                for r in range(height):
                    term = rows[r + a] * factor
                    sums[r] = term if sums[r] is None else sums[r] + term
        for r in range(height):
            out[r, pl.ds(start, EDGE), :] = sums[r]
        return carry

    lax.fori_loop(0, width // EDGE, block, 0)


def kernel_grad(grad_pad, pad, small, height, width):
    channels = pad.shape[2]
    for b in range(TAPS):
        offset = EDGE - HALF + b

        def block(column, sums):
            start = pl.multiple_of(column * EDGE, EDGE)
            near = pad.at[:, pl.ds(start, 3 * EDGE), :]
            rows = [near[r, offset : offset + EDGE, :] for r in range(height + 2 * HALF)]
            grads = [
                grad_pad[r + HALF, pl.ds(pl.multiple_of(start + EDGE, EDGE), EDGE), :]
                for r in range(height)
            ]
            sums = list(sums)
            for a in range(TAPS):
                for r in range(height):
                    sums[a] = sums[a] + grads[r] * rows[r + a]
            return tuple(sums)

        zero = jnp.zeros((EDGE, channels), jnp.float32)
        sums = lax.fori_loop(0, width // EDGE, block, (zero,) * TAPS)
        for a in range(TAPS):
            small[pl.ds(a * TAPS + b, 1), :] = jnp.sum(sums[a], axis=0, keepdims=True)


def owner_of(piece, shift, total):
    return (piece * STRIDE + shift) % total


class Summing:
    def __init__(self, shift, inverse, source, result, send, recv, sems):
        self.lat, self.lon, self.lats, self.lons = here()
        self.total = self.lats * self.lons
        self.me = self.lat * self.lons + self.lon
        self.shift = shift
        self.pieces = source.shape[0] // ROWS
        self.mine = ((self.me + self.total - shift) * inverse) % self.total
        self.source, self.result, self.send, self.recv = source, result, send, recv
        self.sems = [sems.at[k] for k in range(4)]

    def place(self, device):
        return {"lat": device // self.lons, "lon": device % self.lons}

    def rows(self, piece):
        return pl.ds(pl.multiple_of(piece * ROWS, ROWS), ROWS)

    def scatter(self):
        def one(piece, carry):
            owner = owner_of(piece, self.shift, self.total)

            @pl.when(owner != self.me)
            def _():
                slot = (self.me - owner + self.total) % self.total - 1
                pltpu.make_async_remote_copy(
                    src_ref=self.source.at[self.rows(piece)],
                    dst_ref=self.recv.at[self.rows(slot)],
                    send_sem=self.sems[0],
                    recv_sem=self.sems[1],
                    device_id=self.place(owner),
                    device_id_type=MESH,
                ).start()

            return carry

        lax.fori_loop(0, self.pieces, one, 0)

    def gather(self):
        @pl.when(self.mine < self.pieces)
        def _():
            pltpu.make_async_copy(self.recv, self.recv, self.sems[1]).wait()
            own = self.source[self.rows(self.mine)].astype(jnp.float32)
            others = self.recv[...].astype(jnp.float32).reshape(self.total - 1, ROWS, 128)
            self.send[...] = (own + jnp.sum(others, axis=0)).astype(jnp.bfloat16)
            self.result[self.rows(self.mine)] = self.send[...]

            def one(step, carry):
                pltpu.make_async_remote_copy(
                    src_ref=self.send,
                    dst_ref=self.result.at[self.rows(self.mine)],
                    send_sem=self.sems[2],
                    recv_sem=self.sems[3],
                    device_id=self.place((self.me + step) % self.total),
                    device_id_type=MESH,
                ).start()
                return carry

            lax.fori_loop(1, self.total, one, 0)

    def finish(self):
        @pl.when(self.mine < self.pieces)
        def _():
            part = self.source.at[pl.ds(0, (self.pieces - 1) * ROWS)]
            pltpu.make_async_copy(part, part, self.sems[0]).wait()
            out_part = self.result.at[pl.ds(0, (self.pieces - 1) * ROWS)]
            pltpu.make_async_copy(out_part, out_part, self.sems[3]).wait()
            pltpu.make_async_copy(self.recv, self.recv, self.sems[2]).wait()

        @pl.when(self.mine >= self.pieces)
        def _():
            pltpu.make_async_copy(self.source, self.source, self.sems[0]).wait()
            pltpu.make_async_copy(self.result, self.result, self.sems[3]).wait()


def backward_kernel(
    inverse,
    pad, dense, cotangent, mask, kernel_ref, gain_ref, w_in, w_in_t, w_out_t, embed, proj_t,
    state_out, embed_out, early_out, late_out,
    wide_kernel, conv, grad_pad, state_low, g_window, grad_in, grad_out, small, gain_sum,
    back_out, back_in, top_out, bottom_out, top_in, bottom_in,
    early_send, early_one, early_recv, late_send, late_one, late_recv,
    halo_send, halo_recv, back_send, back_recv, early_sems, late_sems,
):
    lat, lon, lats, lons = here()
    total = lats * lons
    me = lat * lons + lon
    height, width, channels = cotangent.shape
    hidden = w_in.shape[1]
    cells = embed.shape[0]
    barrier = pltpu.get_barrier_semaphore()

    def greet(step, carry):
        device = (me + step) % total
        pl.semaphore_signal(
            barrier, inc=1, device_id={"lat": device // lons, "lon": device % lons},
            device_id_type=MESH,
        )
        return carry

    lax.fori_loop(1, total, greet, 0)
    for tap in range(TAPS * TAPS):
        wide_kernel[tap] = jnp.broadcast_to(kernel_ref[tap : tap + 1, :], (EDGE, channels))
    depthwise(pad, wide_kernel, conv, height, width, False)
    grad_in[...] = jnp.zeros(grad_in.shape, jnp.float32)
    grad_out[...] = jnp.zeros(grad_out.shape, jnp.float32)
    gain_sum[...] = jnp.zeros(gain_sum.shape, jnp.float32)
    gain = gain_ref[...]
    piece = 256
    c0 = 0.7978845608028654
    c1 = c0 * 0.044715

    def row_step(row, carry):
        field = conv[row]
        center = field - jnp.mean(field, axis=-1, keepdims=True)
        variance = jnp.mean(center * center, axis=-1, keepdims=True)
        inv = lax.rsqrt(variance + EPSILON)
        normed = center * inv
        ln = (normed * gain).astype(jnp.bfloat16)
        sea = jnp.transpose(
            jnp.broadcast_to(mask[pl.ds(row, 1), :].astype(jnp.float32), (channels, width))
        )
        g_y = (cotangent[row].astype(jnp.float32) * sea).astype(jnp.bfloat16)
        g_ln = None
        for start in range(0, hidden, piece):
            part = slice(start, start + piece)
            pre = jnp.dot(ln, w_in[:, part], preferred_element_type=jnp.float32)
            g_hid = jnp.dot(g_y, w_out_t[:, part], preferred_element_type=jnp.float32)
            square = pre * pre
            half = 0.5 + 0.5 * jnp.tanh(pre * (c0 + c1 * square))
            hid = (pre * half).astype(jnp.bfloat16)
            slope = half + pre * (2.0 * half * (1.0 - half)) * (c0 + (3.0 * c1) * square)
            g_pre = (g_hid * slope).astype(jnp.bfloat16)
            grad_in[:, part] += lax.dot_general(
                ln, g_pre, (((0,), (0,)), ((), ())), preferred_element_type=jnp.float32
            )
            grad_out[:, part] += lax.dot_general(
                g_y, hid, (((0,), (0,)), ((), ())), preferred_element_type=jnp.float32
            )
            term = jnp.dot(g_pre, w_in_t[part, :], preferred_element_type=jnp.float32)
            g_ln = term if g_ln is None else g_ln + term
        both = g_ln * normed
        gain_sum[...] += jnp.sum(both.reshape(width // EDGE, EDGE, channels), axis=0)
        g_n = g_ln * gain
        g_conv = (
            g_n
            - jnp.mean(g_n, axis=-1, keepdims=True)
            - normed * jnp.mean(both * gain, axis=-1, keepdims=True)
        ) * inv
        grad_pad[row + HALF, pl.ds(EDGE, width)] = g_conv
        return carry

    lax.fori_loop(0, height, row_step, 0)
    pl.semaphore_wait(barrier, total - 1)
    rims = (grad_pad, top_out, bottom_out, top_in, bottom_in, halo_send, halo_recv)
    halo_start(*rims)

    small[...] = jnp.zeros(small.shape, jnp.float32)
    kernel_grad(grad_pad, pad, small, height, width)
    small[pl.ds(TAPS * TAPS, 1), :] = jnp.sum(gain_sum[...], axis=0, keepdims=True)
    blocks = hidden // channels
    for k in range(blocks):
        columns = slice(k * channels, (k + 1) * channels)
        early_send[pl.ds(k * channels, channels)] = grad_in[:, columns].astype(jnp.bfloat16)
        early_send[pl.ds((blocks + k) * channels, channels)] = grad_out[:, columns].astype(
            jnp.bfloat16
        )
    early_send[pl.ds(2 * blocks * channels, small.shape[0])] = small[...].astype(jnp.bfloat16)
    early = Summing(0, inverse, early_send, early_out, early_one, early_recv, early_sems)
    early.scatter()
    halo_finish(*rims)

    depthwise(grad_pad, wide_kernel, conv, height, width, True)

    def state_step(row, carry):
        state = conv[row] + cotangent[row].astype(jnp.float32)
        state_out[row] = state
        state_low[pl.ds(pl.multiple_of(row * width, 128), width)] = state.astype(jnp.bfloat16)
        return carry

    lax.fori_loop(0, height, state_step, 0)
    early.gather()
    chunk = 256

    def window_step(index, carry):
        at = pl.ds(pl.multiple_of(index * chunk, chunk), chunk)
        g_window[at] = jnp.dot(dense[at, :], state_low[...], preferred_element_type=jnp.float32)
        return carry

    lax.fori_loop(cells // chunk, 2 * cells // chunk, window_step, 0)
    back_out[...] = g_window[pl.ds(cells, cells)].astype(jnp.bfloat16)
    back = pltpu.make_async_remote_copy(
        src_ref=back_out, dst_ref=back_in, send_sem=back_send, recv_sem=back_recv,
        device_id={"lat": lat + 1, "lon": lon}, device_id_type=MESH,
    )
    pl.when(lat < lats - 1)(back.start)
    lax.fori_loop(0, cells // chunk, window_step, 0)

    @pl.when(lat > 0)
    def _():
        back.wait_recv()
        g_window[pl.ds(0, cells)] += back_in[...].astype(jnp.float32)

    pl.when(lat < lats - 1)(back.wait_send)
    g_own = g_window[pl.ds(0, cells)].astype(jnp.bfloat16)
    late_send[...] = lax.dot_general(
        embed[...], g_own, (((0,), (0,)), ((), ())), preferred_element_type=jnp.float32
    ).astype(jnp.bfloat16)
    late = Summing(1, inverse, late_send, late_out, late_one, late_recv, late_sems)
    late.scatter()
    embed_out[...] = jnp.dot(g_own, proj_t[...], preferred_element_type=jnp.float32)
    late.gather()
    early.finish()
    late.finish()


def backward(pad, dense, cotangent, mask, kernel, gain, w_in, w_out, embed, projection):
    height, width, channels = cotangent.shape
    hidden = w_in.shape[1]
    cells, features = embed.shape
    total = lax.axis_size("lat") * lax.axis_size("lon")
    small_rows = -(-(TAPS * TAPS + 1) // ROWS) * ROWS
    early_rows = 2 * hidden * channels // 128 + small_rows
    late_rows = features * channels // 128
    low = jnp.bfloat16
    full = jnp.float32
    rim = VMEM((HALF, width, channels), low)
    dma = pltpu.SemaphoreType.DMA
    return pl.pallas_call(
        functools.partial(backward_kernel, pow(STRIDE, -1, total)),
        out_shape=(
            jax.ShapeDtypeStruct((height, width, channels), full),
            jax.ShapeDtypeStruct((cells, features), full),
            jax.ShapeDtypeStruct((early_rows, 128), low),
            jax.ShapeDtypeStruct((late_rows, 128), low),
        ),
        in_specs=[pl.BlockSpec(memory_space=VMEM)] * 11,
        out_specs=(pl.BlockSpec(memory_space=VMEM),) * 4,
        scratch_shapes=[
            VMEM((TAPS * TAPS, EDGE, channels), full),
            VMEM((height, width, channels), full),
            VMEM((height + 2 * HALF, width + 2 * EDGE, channels), full),
            VMEM((height * width, channels), low),
            VMEM((2 * cells, channels), full),
            VMEM((channels, hidden), full),
            VMEM((channels, hidden), full),
            VMEM((small_rows, channels), full),
            VMEM((EDGE, channels), full),
            VMEM((cells, channels), low),
            VMEM((cells, channels), low),
            rim, rim, rim, rim,
            VMEM((early_rows, 128), low),
            VMEM((ROWS, 128), low),
            VMEM(((total - 1) * ROWS, 128), low),
            VMEM((late_rows, 128), low),
            VMEM((ROWS, 128), low),
            VMEM(((total - 1) * ROWS, 128), low),
            dma((8,)), dma((8,)), dma(()), dma(()), dma((4,)), dma((4,)),
        ],
        compiler_params=pltpu.CompilerParams(
            collective_id=1, has_side_effects=True, vmem_limit_bytes=LIMIT
        ),
    )(
        pad, dense, cotangent, mask, kernel.reshape(TAPS * TAPS, channels),
        gain.reshape(1, channels), w_in, w_in.T, w_out.T, embed, projection.T,
    )


def unpack_kernel(early, late, grad_projection, grad_kernel, grad_gain, grad_in, grad_out):
    channels, hidden = grad_in.shape
    blocks = hidden // channels
    grad_projection[...] = late[...].astype(jnp.float32)
    for k in range(blocks):
        columns = slice(k * channels, (k + 1) * channels)
        grad_in[:, columns] = early[pl.ds(k * channels, channels)].astype(jnp.float32)
        grad_out[columns, :] = jnp.transpose(
            early[pl.ds((blocks + k) * channels, channels)].astype(jnp.float32)
        )
    first = 2 * blocks * channels
    small = early[pl.ds(first, early.shape[0] - first)].astype(jnp.float32)
    for a in range(TAPS):
        grad_kernel[a] = small[a * TAPS : (a + 1) * TAPS]
    grad_gain[...] = small[TAPS * TAPS : TAPS * TAPS + 1]


def unpack(early, late, channels, hidden, features):
    shapes = (
        (features, channels), (TAPS, TAPS, channels), (1, channels),
        (channels, hidden), (hidden, channels),
    )
    return pl.pallas_call(
        unpack_kernel,
        out_shape=tuple(jax.ShapeDtypeStruct(shape, jnp.float32) for shape in shapes),
        in_specs=[pl.BlockSpec(memory_space=VMEM)] * 2,
        out_specs=(pl.BlockSpec(memory_space=VMEM),) * 5,
        compiler_params=pltpu.CompilerParams(vmem_limit_bytes=8 << 20),
    )(early, late)


def shards(
    ocean_state,
    cotangent,
    atm_embed,
    projection,
    dw_kernel,
    norm_gain,
    w_in,
    w_out,
    margin_index,
    margin_weight,
    sea_mask,
):
    channels, hidden = w_in.shape
    pad, dense = forward(atm_embed, projection, margin_index, margin_weight, ocean_state)
    grad_state, grad_embed, early, late = backward(
        pad, dense, cotangent, sea_mask, dw_kernel, norm_gain, w_in, w_out, atm_embed, projection
    )
    grad_projection, grad_kernel, grad_gain, grad_in, grad_out = unpack(
        early, late, channels, hidden, atm_embed.shape[1]
    )
    return (
        grad_state, grad_embed, grad_projection, grad_kernel,
        grad_gain.reshape(channels), grad_in, grad_out,
    )


def solution(mesh):
    return jax.shard_map(
        shards,
        mesh=mesh,
        in_specs=(
            P("lat", "lon", None),
            P("lat", "lon", None),
            P(("lat", "lon"), None),
            P(),
            P(),
            P(),
            P(),
            P(),
            P(None, "lat", "lon"),
            P(None, "lat", "lon"),
            P("lat", "lon"),
        ),
        out_specs=(P("lat", "lon", None), P(("lat", "lon"), None), P(), P(), P(), P(), P()),
        check_vma=False,
    )
```

time: 304 us -> 92.5 us (0.30)
  waiting for transfers between devices: 88.6 us -> 0 us
  blocking collectives: 79.5 us -> 0 us
  Pallas kernels: 0 us -> 79 us
  matrix products: 54 us -> 0 us
  other arithmetic: 36.5 us -> 0 us
  starting transfers between devices: 16.7 us -> 0 us
  between operations: 16 us -> 0.71 us
    psum x1 -> x0, blocking collectives: 79.5 us -> none  [shards(): lax.psum((partials[0], partials[1], partials[2], partials[3], partials[4]...]
    pallas_call x0 -> x3, Pallas kernels: none -> 79 us  [the longest x1 60.3 us: backward(): pl.pallas_call(functools.partial(backward_kernel, pow(STRIDE, -1, total))...]
    psum x1 -> x0, waiting for transfers between devices: 76.1 us -> none  [shards(): lax.psum((partials[0], partials[1], partials[2], partials[3], partials[4]...]
    dot_general x14 -> x0, matrix products: 54 us -> none  [the longest x3 22.6 us: backward_block(): lax.dot_general(dense, triple[2], (((0,), (0,)), ((), ())), precision=lax...]
    reduce_sum x6 -> x0, other arithmetic: 21.4 us -> none  [the longest x3 9.44 us: kernel_grad(): jnp.sum(grad * padded[row_tap:row_tap + height, col_tap:col_tap + width],...]
    ppermute x10 -> x0, starting transfers between devices: 16.7 us -> none  [the longest x4 6.95 us: with_halo(): lax.ppermute(lax.slice_in_dim(block, 0, width, axis=dim), axis, backward)]
    ppermute x10 -> x0, waiting for transfers between devices: 12.5 us -> none  [the longest x4 4.69 us: with_halo(): lax.ppermute(lax.slice_in_dim(block, block.shape[dim] - width, None, axis...]
    add x3 -> x0, other arithmetic: 12.1 us -> none  [the longest x1 8.94 us: shards(): grad_state = g_out + depthwise_back(g_padded, dw_kernel)]
  transfers between devices with their start and end apart: 11 -> 0, of which waited for: 7 -> 0; matrix products, arithmetic and copies ran while one was open for 4% -> 0% of each run, Pallas kernels for 0% -> 0%
where the time goes in v2:
time: 92.5 us; the launch traced here: 92 us
  Pallas kernels  79 us (85%)
  local copies, waits for them, and re-layouts  12.3 us (13%)
    pallas_call x1, Pallas kernels, backward(): pl.pallas_call(functools.partial(backward_kernel, pow(STRIDE, -1, total))...  60.3 us
    pallas_call x1, Pallas kernels, forward(): pl.pallas_call(forward_kernel, out_shape=(jax.ShapeDtypeStruct((height +...  17.8 us
    unnamed x21, local copies, waits for them, and re-layouts  11.5 us

profile of v2, /device:TPU:1, one launch (start us, length us, event | category | flops | bytes accessed | tf_op | source)
XLA Modules:
  0.0 92.0 jit_solution(13559530305069456618)
XLA Ops:
  0.6 0.0 copy-start.2
  0.6 0.8 reshape.23.kernel_ref
  1.5 0.8 copy.18.index_ref
  2.2 0.8 copy.19.weight_ref
  3.0 0.9 %copy.22 = bf16[256,128]{0,1:T(8,128)(2,1)S(1)} copy(bf16[256,128]{1,0:T(8,128)(2,1)} %proj_ref.1) | data formatting | bytes 131072 | tf_op args[3]
  4.0 1.0 %copy.21 = bf16[512,128]{0,1:T(8,128)(2,1)S(1)} copy(bf16[512,128]{1,0:T(8,128)(2,1)} %param.18) | data formatting | bytes 262144 | tf_op args[7]
  5.0 1.0 %copy.20 = bf16[128,512]{0,1:T(8,128)(2,1)S(1)} copy(bf16[128,512]{1,0:T(8,128)(2,1)} %w_in.1) | data formatting | bytes 262144 | tf_op args[6]
  6.0 0.0 copy-start
  6.0 0.9 %copy-done = bf16[512,256]{1,0:T(8,128)(2,1)S(1)} copy-done((bf16[512,256]{1,0:T(8,128)(2,1)S(1)}, bf16[512,256]{1,0:T(8,128)(2,1)}, u32[]{:S(2)}) %copy-start) | copy-done | bytes 262168
  7.0 0.0 copy-start.1
  7.0 1.1 %copy-done.1 = bf16[9,256,128]{2,1,0:T(8,128)(2,1)S(1)} copy-done((bf16[9,256,128]{2,1,0:T(8,128)(2,1)S(1)}, bf16[9,256,128]{2,1,0:T(8,128)(2,1)}, u32[]{:S(2)}) %copy-start.1) | copy-done | bytes 589848
  8.0 0.0 copy-start.4
  8.0 0.8 copy-done.4
  8.9 17.8 %shard_map.162 = (f32[15,272,128]{2,1,0:T(8,128)S(1)}, bf16[1024,2304]{1,0:T(8,128)(2,1)S(1)}) custom-call(bf16[512,256]{1,0:T(8,128)(2,1)S(1)} %copy-done, bf16[256,128]{1,0:T(8,128)(2,1)S(1)} %copy-done.4, s32[4,9,256]{2,1,0:T(8,128)S(1)} %copy.18.index_ref, f32[4,9,256]{2,1,0:T(8,128)S(1)} %copy.19.weight_ref, bf16[9,256,128]{2,1,0:T(8,128)(2,1)S(1)} %copy-done.1), custom_call_target="tpu_custom_call" | custom-call | tf_op jit(solution)/shard_map/pallas_call | solution.py:206
  26.7 0.0 copy-done.2
  26.7 0.0 copy-start.3
  26.7 0.9 copy-done.3
  27.6 0.0 copy-start.5
  27.6 0.7 copy-done.5
  28.3 0.0 copy-start.6
  28.4 0.7 copy-done.6
  29.0 60.3 %shard_map.163 = (f32[9,256,128]{2,1,0:T(8,128)S(1)}, f32[512,256]{1,0:T(8,128)S(1)}, bf16[1088,128]{1,0:T(8,128)(2,1)S(1)}, bf16[256,128]{1,0:T(8,128)(2,1)S(1)}) custom-call(f32[15,272,128]{2,1,0:T(8,128)S(1)} %get-tuple-element.18.pad, bf16[1024,2304]{1,0:T(8,128)(2,1)S(1)} %get-tuple-element.19.dense, bf16[9,256,128]{2,1,0:T(8,128)(2,1)S(1)} %copy-done.2, ...), custom_call_target="tpu_custom_call" | custom-call | tf_op jit(solution)/shard_map/pallas_call | solution.py:506
  89.3 0.9 shard_map.164
  90.2 1.0 %copy.25 = f32[9,256,128]{2,1,0:T(8,128)} copy(f32[9,256,128]{2,1,0:T(8,128)S(1)} %get-tuple-element.36) | data formatting | bytes 2359296
  91.2 0.8 copy.26
Async XLA Ops:
  0.6 26.1 %copy-start.2 = (bf16[9,256,128]{2,1,0:T(8,128)(2,1)S(1)}, bf16[9,256,128]{2,1,0:T(8,128)(2,1)}, u32[]{:S(2)}) copy-start(bf16[9,256,128]{2,1,0:T(8,128)(2,1)} %cotangent.1) | copy-start | bytes 1769476
  6.0 1.0 %copy-start = (bf16[512,256]{1,0:T(8,128)(2,1)S(1)}, bf16[512,256]{1,0:T(8,128)(2,1)}, u32[]{:S(2)}) copy-start(bf16[512,256]{1,0:T(8,128)(2,1)} %embed.1) | copy-start | bytes 786436
  7.0 1.1 %copy-start.1 = (bf16[9,256,128]{2,1,0:T(8,128)(2,1)S(1)}, bf16[9,256,128]{2,1,0:T(8,128)(2,1)}, u32[]{:S(2)}) copy-start(bf16[9,256,128]{2,1,0:T(8,128)(2,1)} %state_ref.1) | copy-start | bytes 1769476
  8.0 0.8 copy-start.4
  26.7 0.9 copy-start.3
  27.6 0.7 copy-start.5
  28.3 0.7 copy-start.6

commit v3 on v2

--- a/solution.py
+++ b/solution.py
@@ -14,7 +14,7 @@
 HALF = 3
 MESH = pl.DeviceIdType.MESH
 VMEM = pltpu.VMEM
-LIMIT = 28 << 20
+LIMIT = 60 << 20
 
 
 def here():
@@ -112,118 +112,115 @@
         pad[pl.ds(HALF + height, HALF), inner] = bottom_in[...].astype(jnp.float32)
 
 
-def forward_kernel(
-    embed_ref, proj_ref, index_ref, weight_ref, state_ref, pad, dense,
+def fetch(sources, targets, sems):
+    copies = [
+        pltpu.make_async_copy(source, target, sems.at[number])
+        for number, (source, target) in enumerate(zip(sources, targets))
+    ]
+    for copy in copies:
+        copy.start()
+    return copies
+
+
+def greet_all(barrier):
+    lat, lon, lats, lons = here()
+    columns = [lax.rem(lon + step, lons) for step in range(lons)]
+
+    def one(step, carry):
+        row = lax.rem(lat + step, lats)
+        for number, column in enumerate(columns):
+            def send(column=column):
+                pl.semaphore_signal(
+                    barrier, inc=1, device_id={"lat": row, "lon": column}, device_id_type=MESH
+                )
+
+            guarded(step > 0 if number == 0 else None, send)
+        return carry
+
+    lax.fori_loop(0, lats, one, 0)
+
+
+def forward_part(
+    barrier, embed_ref, index_ref, weight_ref, state_ref, proj_ref, loads, pad, dense, next_embed,
     own, following, top_out, bottom_out, top_in, bottom_in,
-    send_sem, recv_sem, window_send, window_recv,
+    send_sem, recv_sem, window_send, window_recv, embed_send, embed_recv,
 ):
     lat, lon, lats, lons = here()
-    margins, height, width = index_ref.shape
+    height, margins, width = index_ref.shape
     cells = embed_ref.shape[0]
     slots = 2 * cells
-    left = (lon + lons - 1) % lons
-    right = (lon + 1) % lons
-    barrier = pltpu.get_barrier_semaphore()
-
-    def greet(to_lat, to_lon):
-        pl.semaphore_signal(
-            barrier, inc=1, device_id={"lat": to_lat, "lon": to_lon}, device_id_type=MESH
-        )
-
-    greet(lat, left)
-    greet(lat, right)
-
-    @pl.when(lat > 0)
-    def _():
-        for to_lon in (left, lon, right):
-            greet(lat - 1, to_lon)
-
-    @pl.when(lat < lats - 1)
-    def _():
-        for to_lon in (left, lon, right):
-            greet(lat + 1, to_lon)
-
-    projected = jnp.dot(embed_ref[...], proj_ref[...], preferred_element_type=jnp.float32)
-    own[...] = jnp.transpose(projected).astype(jnp.bfloat16)
-    ends = (lat == 0).astype(jnp.int32) + (lat == lats - 1).astype(jnp.int32)
-    pl.semaphore_wait(barrier, 8 - 3 * ends)
-
-    window = pltpu.make_async_remote_copy(
-        src_ref=own, dst_ref=following, send_sem=window_send, recv_sem=window_recv,
-        device_id={"lat": lat - 1, "lon": lon}, device_id_type=MESH,
-    )
-    pl.when(lat > 0)(window.start)
-
+    index_load, weight_load, embed_load, proj_load, state_load = loads
+    index_load.wait()
+    weight_load.wait()
     step = 32
     base = lax.broadcasted_iota(jnp.int32, (step, width), 0)
 
     def build(row, carry):
-        picks = [index_ref[q, pl.ds(row, 1), :] for q in range(margins)]
-        loads = [weight_ref[q, pl.ds(row, 1), :] for q in range(margins)]
+        indices = index_ref[row]
+        factors = weight_ref[row]
+        picks = [indices[q : q + 1, :] for q in range(margins)]
+        weights = [factors[q : q + 1, :] for q in range(margins)]
         at = pl.ds(pl.multiple_of(row * width, 128), width)
         for start in range(0, slots, step):
             here_slots = base + start
             total = None
-            for pick, load in zip(picks, loads):
-                term = jnp.where(here_slots == pick, load, 0.0)
+            for pick, weight in zip(picks, weights):
+                term = jnp.where(here_slots == pick, weight, 0.0)
                 total = term if total is None else total + term
             dense[pl.ds(start, step), at] = total.astype(jnp.bfloat16)
         return carry
 
     lax.fori_loop(0, height, build, 0)
+
+    embed_load.wait()
+    proj_load.wait()
+    projected = jnp.dot(embed_ref[...], proj_ref[...], preferred_element_type=jnp.float32)
+    own[...] = jnp.transpose(projected).astype(jnp.bfloat16)
+    pl.semaphore_wait(barrier, lats * lons - 1)
+    window = pltpu.make_async_remote_copy(
+        src_ref=own, dst_ref=following, send_sem=window_send, recv_sem=window_recv,
+        device_id={"lat": lat - 1, "lon": lon}, device_id_type=MESH,
+    )
+    ahead = pltpu.make_async_remote_copy(
+        src_ref=embed_ref, dst_ref=next_embed, send_sem=embed_send, recv_sem=embed_recv,
+        device_id={"lat": lat - 1, "lon": lon}, device_id_type=MESH,
+    )
+    pl.when(lat > 0)(window.start)
+    state_load.wait()
+
+    def force_own(row, carry):
+        at = pl.ds(pl.multiple_of(row * width, 128), width)
+        forcing = jnp.dot(own[...], dense[pl.ds(0, cells), at], preferred_element_type=jnp.float32)
+        pad[row + HALF, pl.ds(EDGE, width)] = (
+            state_ref[row].astype(jnp.float32) + jnp.transpose(forcing)
+        )
+        return carry
+
+    lax.fori_loop(0, height, force_own, 0)
+
+    @pl.when(lat == lats - 1)
+    def _():
+        next_embed[...] = jnp.zeros(next_embed.shape, jnp.bfloat16)
+
+    def force_next(row, carry):
+        at = pl.ds(pl.multiple_of(row * width, 128), width)
+        forcing = jnp.dot(
+            following[...], dense[pl.ds(cells, cells), at], preferred_element_type=jnp.float32
+        )
+        pad[row + HALF, pl.ds(EDGE, width)] += jnp.transpose(forcing)
+        return carry
 
     @pl.when(lat < lats - 1)
     def _():
         window.wait_recv()
-
-    @pl.when(lat == lats - 1)
-    def _():
-        following[...] = jnp.zeros(following.shape, jnp.bfloat16)
+        lax.fori_loop(0, height, force_next, 0)
 
     pl.when(lat > 0)(window.wait_send)
-
-    def force(row, carry):
-        at = pl.ds(pl.multiple_of(row * width, 128), width)
-        forcing = jnp.dot(own[...], dense[pl.ds(0, cells), at], preferred_element_type=jnp.float32)
-        forcing = forcing + jnp.dot(
-            following[...], dense[pl.ds(cells, cells), at], preferred_element_type=jnp.float32
-        )
-        pad[row + HALF, pl.ds(EDGE, width)] = (
-            state_ref[row].astype(jnp.float32) + jnp.transpose(forcing)
-        )
-        return carry
-
-    lax.fori_loop(0, height, force, 0)
     rims = (pad, top_out, bottom_out, top_in, bottom_in, send_sem, recv_sem)
     halo_start(*rims)
+    pl.when(lat > 0)(ahead.start)
     halo_finish(*rims)
-
-
-def forward(embed, projection, index, weight, state):
-    height, width, channels = state.shape
-    slots = 2 * embed.shape[0]
-    rim = VMEM((HALF, width, channels), jnp.bfloat16)
-    return pl.pallas_call(
-        forward_kernel,
-        out_shape=(
-            jax.ShapeDtypeStruct((height + 2 * HALF, width + 2 * EDGE, channels), jnp.float32),
-            jax.ShapeDtypeStruct((slots, height * width), jnp.bfloat16),
-        ),
-        in_specs=[pl.BlockSpec(memory_space=VMEM)] * 5,
-        out_specs=(pl.BlockSpec(memory_space=VMEM),) * 2,
-        scratch_shapes=[
-            VMEM((channels, embed.shape[0]), jnp.bfloat16),
-            VMEM((channels, embed.shape[0]), jnp.bfloat16),
-            rim, rim, rim, rim,
-            pltpu.SemaphoreType.DMA((8,)),
-            pltpu.SemaphoreType.DMA((8,)),
-            pltpu.SemaphoreType.DMA(()),
-            pltpu.SemaphoreType.DMA(()),
-        ],
-        compiler_params=pltpu.CompilerParams(
-            collective_id=0, has_side_effects=True, vmem_limit_bytes=LIMIT
-        ),
-    )(embed, projection, index, weight, state)
+    return ahead
 
 
 def depthwise(pad, wide_kernel, out, height, width, flipped):
@@ -273,7 +270,7 @@
 
 
 def owner_of(piece, shift, total):
-    return (piece * STRIDE + shift) % total
+    return lax.rem(piece * STRIDE + shift, total)
 
 
 class Summing:
@@ -283,12 +280,12 @@
         self.me = self.lat * self.lons + self.lon
         self.shift = shift
         self.pieces = source.shape[0] // ROWS
-        self.mine = ((self.me + self.total - shift) * inverse) % self.total
+        self.mine = lax.rem((self.me + self.total - shift) * inverse, self.total)
         self.source, self.result, self.send, self.recv = source, result, send, recv
         self.sems = [sems.at[k] for k in range(4)]
 
     def place(self, device):
-        return {"lat": device // self.lons, "lon": device % self.lons}
+        return {"lat": lax.div(device, self.lons), "lon": lax.rem(device, self.lons)}
 
     def rows(self, piece):
         return pl.ds(pl.multiple_of(piece * ROWS, ROWS), ROWS)
@@ -299,7 +296,7 @@
 
             @pl.when(owner != self.me)
             def _():
-                slot = (self.me - owner + self.total) % self.total - 1
+                slot = lax.rem(self.me - owner + self.total, self.total) - 1
                 pltpu.make_async_remote_copy(
                     src_ref=self.source.at[self.rows(piece)],
                     dst_ref=self.recv.at[self.rows(slot)],
@@ -322,18 +319,23 @@
             self.send[...] = (own + jnp.sum(others, axis=0)).astype(jnp.bfloat16)
             self.result[self.rows(self.mine)] = self.send[...]
 
+            columns = [lax.rem(self.lon + step, self.lons) for step in range(self.lons)]
+
             def one(step, carry):
-                pltpu.make_async_remote_copy(
-                    src_ref=self.send,
-                    dst_ref=self.result.at[self.rows(self.mine)],
-                    send_sem=self.sems[2],
-                    recv_sem=self.sems[3],
-                    device_id=self.place((self.me + step) % self.total),
-                    device_id_type=MESH,
-                ).start()
+                row = lax.rem(self.lat + step, self.lats)
+                for number, column in enumerate(columns):
+                    copy = pltpu.make_async_remote_copy(
+                        src_ref=self.send,
+                        dst_ref=self.result.at[self.rows(self.mine)],
+                        send_sem=self.sems[2],
+                        recv_sem=self.sems[3],
+                        device_id={"lat": row, "lon": column},
+                        device_id_type=MESH,
+                    )
+                    guarded(step > 0 if number == 0 else None, copy.start)
                 return carry
 
-            lax.fori_loop(1, self.total, one, 0)
+            lax.fori_loop(0, self.lats, one, 0)
 
     def finish(self):
         @pl.when(self.mine < self.pieces)
@@ -350,34 +352,50 @@
             pltpu.make_async_copy(self.result, self.result, self.sems[3]).wait()
 
 
-def backward_kernel(
-    inverse,
-    pad, dense, cotangent, mask, kernel_ref, gain_ref, w_in, w_in_t, w_out_t, embed, proj_t,
+def whole_kernel(
+    inverse, shift,
+    index_hbm, weight_hbm, embed_hbm, proj_hbm, state_hbm, kernel_hbm, cotangent_hbm, mask_hbm,
+    gain_hbm, w_in_hbm, w_out_hbm,
     state_out, embed_out, early_out, late_out,
+    index_ref, weight_ref, embed, proj, state_in, kernel_ref, cotangent, mask,
+    gain_ref, w_in, w_out,
+    pad, dense, next_embed, own, following, x_top_out, x_bottom_out, x_top_in, x_bottom_in,
+    w_in_t, w_out_t, proj_t,
     wide_kernel, conv, grad_pad, state_low, g_window, grad_in, grad_out, small, gain_sum,
-    back_out, back_in, top_out, bottom_out, top_in, bottom_in,
+    back_out, back_in, g_embed, top_out, bottom_out, top_in, bottom_in,
     early_send, early_one, early_recv, late_send, late_one, late_recv,
-    halo_send, halo_recv, back_send, back_recv, early_sems, late_sems,
+    fetch_sem, x_send, x_recv, window_send, window_recv, ahead_send, ahead_recv,
+    halo_send, halo_recv, back_send, back_recv, early_sems, late_sems, move_sem,
 ):
     lat, lon, lats, lons = here()
-    total = lats * lons
-    me = lat * lons + lon
     height, width, channels = cotangent.shape
     hidden = w_in.shape[1]
-    cells = embed.shape[0]
+    cells, features = embed.shape
+    loads = fetch(
+        (
+            index_hbm, weight_hbm, embed_hbm, proj_hbm, state_hbm, kernel_hbm, cotangent_hbm,
+            mask_hbm, gain_hbm, w_in_hbm, w_out_hbm,
+        ),
+        (
+            index_ref, weight_ref, embed, proj, state_in, kernel_ref, cotangent,
+            mask, gain_ref, w_in, w_out,
+        ),
+        fetch_sem,
+    )
     barrier = pltpu.get_barrier_semaphore()
-
-    def greet(step, carry):
-        device = (me + step) % total
-        pl.semaphore_signal(
-            barrier, inc=1, device_id={"lat": device // lons, "lon": device % lons},
-            device_id_type=MESH,
-        )
-        return carry
-
-    lax.fori_loop(1, total, greet, 0)
+    greet_all(barrier)
+    ahead = forward_part(
+        barrier, embed, index_ref, weight_ref, state_in, proj, loads[:5], pad, dense, next_embed,
+        own, following, x_top_out, x_bottom_out, x_top_in, x_bottom_in,
+        x_send, x_recv, window_send, window_recv, ahead_send, ahead_recv,
+    )
+    for load in loads[5:]:
+        load.wait()
     for tap in range(TAPS * TAPS):
-        wide_kernel[tap] = jnp.broadcast_to(kernel_ref[tap : tap + 1, :], (EDGE, channels))
+        a, b = divmod(tap, TAPS)
+        wide_kernel[tap] = jnp.broadcast_to(kernel_ref[a, b : b + 1, :], (EDGE, channels))
+    for source, target in ((w_in, w_in_t), (w_out, w_out_t), (proj, proj_t)):
+        target[...] = jnp.transpose(source[...].astype(jnp.float32)).astype(jnp.bfloat16)
     depthwise(pad, wide_kernel, conv, height, width, False)
     grad_in[...] = jnp.zeros(grad_in.shape, jnp.float32)
     grad_out[...] = jnp.zeros(grad_out.shape, jnp.float32)
@@ -428,13 +446,9 @@
         return carry
 
     lax.fori_loop(0, height, row_step, 0)
-    pl.semaphore_wait(barrier, total - 1)
     rims = (grad_pad, top_out, bottom_out, top_in, bottom_in, halo_send, halo_recv)
     halo_start(*rims)
 
-    small[...] = jnp.zeros(small.shape, jnp.float32)
-    kernel_grad(grad_pad, pad, small, height, width)
-    small[pl.ds(TAPS * TAPS, 1), :] = jnp.sum(gain_sum[...], axis=0, keepdims=True)
     blocks = hidden // channels
     for k in range(blocks):
         columns = slice(k * channels, (k + 1) * channels)
@@ -442,20 +456,25 @@
         early_send[pl.ds((blocks + k) * channels, channels)] = grad_out[:, columns].astype(
             jnp.bfloat16
         )
-    early_send[pl.ds(2 * blocks * channels, small.shape[0])] = small[...].astype(jnp.bfloat16)
     early = Summing(0, inverse, early_send, early_out, early_one, early_recv, early_sems)
     early.scatter()
+    small[...] = jnp.zeros(small.shape, jnp.float32)
+    kernel_grad(grad_pad, pad, small, height, width)
+    small[pl.ds(TAPS * TAPS, 1), :] = jnp.sum(gain_sum[...], axis=0, keepdims=True)
+    late_send[pl.ds(features, small.shape[0])] = small[...].astype(jnp.bfloat16)
     halo_finish(*rims)
 
     depthwise(grad_pad, wide_kernel, conv, height, width, True)
 
     def state_step(row, carry):
         state = conv[row] + cotangent[row].astype(jnp.float32)
-        state_out[row] = state
+        conv[row] = state
         state_low[pl.ds(pl.multiple_of(row * width, 128), width)] = state.astype(jnp.bfloat16)
         return carry
 
     lax.fori_loop(0, height, state_step, 0)
+    state_move = pltpu.make_async_copy(conv, state_out, move_sem.at[0])
+    state_move.start()
     early.gather()
     chunk = 256
 
@@ -464,14 +483,28 @@
         g_window[at] = jnp.dot(dense[at, :], state_low[...], preferred_element_type=jnp.float32)
         return carry
 
-    lax.fori_loop(cells // chunk, 2 * cells // chunk, window_step, 0)
+    lax.fori_loop(0, 2 * cells // chunk, window_step, 0)
     back_out[...] = g_window[pl.ds(cells, cells)].astype(jnp.bfloat16)
+    pl.when(lat > 0)(ahead.wait_send)
+    pl.when(lat < lats - 1)(ahead.wait_recv)
+    late_send[pl.ds(0, features)] = (
+        lax.dot_general(
+            embed[...], g_window[pl.ds(0, cells)].astype(jnp.bfloat16),
+            (((0,), (0,)), ((), ())), preferred_element_type=jnp.float32,
+        )
+        + lax.dot_general(
+            next_embed[...], back_out[...],
+            (((0,), (0,)), ((), ())), preferred_element_type=jnp.float32,
+        )
+    ).astype(jnp.bfloat16)
+    late = Summing(shift, inverse, late_send, late_out, late_one, late_recv, late_sems)
+    late.scatter()
     back = pltpu.make_async_remote_copy(
         src_ref=back_out, dst_ref=back_in, send_sem=back_send, recv_sem=back_recv,
         device_id={"lat": lat + 1, "lon": lon}, device_id_type=MESH,
     )
     pl.when(lat < lats - 1)(back.start)
-    lax.fori_loop(0, cells // chunk, window_step, 0)
+    late.gather()
 
     @pl.when(lat > 0)
     def _():
@@ -480,43 +513,59 @@
 
     pl.when(lat < lats - 1)(back.wait_send)
     g_own = g_window[pl.ds(0, cells)].astype(jnp.bfloat16)
-    late_send[...] = lax.dot_general(
-        embed[...], g_own, (((0,), (0,)), ((), ())), preferred_element_type=jnp.float32
-    ).astype(jnp.bfloat16)
-    late = Summing(1, inverse, late_send, late_out, late_one, late_recv, late_sems)
-    late.scatter()
-    embed_out[...] = jnp.dot(g_own, proj_t[...], preferred_element_type=jnp.float32)
-    late.gather()
+    g_embed[...] = jnp.dot(g_own, proj_t[...], preferred_element_type=jnp.float32)
+    embed_move = pltpu.make_async_copy(g_embed, embed_out, move_sem.at[1])
+    embed_move.start()
     early.finish()
     late.finish()
-
-
-def backward(pad, dense, cotangent, mask, kernel, gain, w_in, w_out, embed, projection):
+    state_move.wait()
+    embed_move.wait()
+
+
+def whole(index, weight, embed, projection, state, kernel, cotangent, mask, gain, w_in, w_out):
     height, width, channels = cotangent.shape
     hidden = w_in.shape[1]
     cells, features = embed.shape
     total = lax.axis_size("lat") * lax.axis_size("lon")
     small_rows = -(-(TAPS * TAPS + 1) // ROWS) * ROWS
-    early_rows = 2 * hidden * channels // 128 + small_rows
-    late_rows = features * channels // 128
+    early_rows = 2 * hidden * channels // 128
+    late_rows = features * channels // 128 + small_rows
     low = jnp.bfloat16
     full = jnp.float32
     rim = VMEM((HALF, width, channels), low)
+    padded = VMEM((height + 2 * HALF, width + 2 * EDGE, channels), full)
     dma = pltpu.SemaphoreType.DMA
+    fetched = (
+        index, weight, embed, projection, state, kernel, cotangent, mask,
+        gain.reshape(1, channels), w_in, w_out,
+    )
     return pl.pallas_call(
-        functools.partial(backward_kernel, pow(STRIDE, -1, total)),
+        functools.partial(
+            whole_kernel, pow(STRIDE, -1, total), early_rows // ROWS * STRIDE % total
+        ),
         out_shape=(
             jax.ShapeDtypeStruct((height, width, channels), full),
             jax.ShapeDtypeStruct((cells, features), full),
             jax.ShapeDtypeStruct((early_rows, 128), low),
             jax.ShapeDtypeStruct((late_rows, 128), low),
         ),
-        in_specs=[pl.BlockSpec(memory_space=VMEM)] * 11,
-        out_specs=(pl.BlockSpec(memory_space=VMEM),) * 4,
-        scratch_shapes=[
+        in_specs=[pl.BlockSpec(memory_space=pltpu.HBM)] * len(fetched),
+        out_specs=(pl.BlockSpec(memory_space=pltpu.HBM),) * 2
+        + (pl.BlockSpec(memory_space=VMEM),) * 2,
+        scratch_shapes=[VMEM(array.shape, array.dtype) for array in fetched]
+        + [
+            padded,
+            VMEM((2 * cells, height * width), low),
+            VMEM((cells, features), low),
+            VMEM((channels, cells), low),
+            VMEM((channels, cells), low),
+            rim, rim, rim, rim,
+            VMEM((hidden, channels), low),
+            VMEM((channels, hidden), low),
+            VMEM((channels, features), low),
             VMEM((TAPS * TAPS, EDGE, channels), full),
             VMEM((height, width, channels), full),
-            VMEM((height + 2 * HALF, width + 2 * EDGE, channels), full),
+            padded,
             VMEM((height * width, channels), low),
             VMEM((2 * cells, channels), full),
             VMEM((channels, hidden), full),
@@ -525,6 +574,7 @@
             VMEM((EDGE, channels), full),
             VMEM((cells, channels), low),
             VMEM((cells, channels), low),
+            VMEM((cells, features), full),
             rim, rim, rim, rim,
             VMEM((early_rows, 128), low),
             VMEM((ROWS, 128), low),
@@ -532,46 +582,59 @@
             VMEM((late_rows, 128), low),
             VMEM((ROWS, 128), low),
             VMEM(((total - 1) * ROWS, 128), low),
-            dma((8,)), dma((8,)), dma(()), dma(()), dma((4,)), dma((4,)),
+            dma((len(fetched),)), dma((8,)), dma((8,)), dma(()), dma(()), dma(()), dma(()),
+            dma((8,)), dma((8,)), dma(()), dma(()), dma((4,)), dma((4,)), dma((2,)),
         ],
         compiler_params=pltpu.CompilerParams(
-            collective_id=1, has_side_effects=True, vmem_limit_bytes=LIMIT
+            collective_id=0, has_side_effects=True, vmem_limit_bytes=LIMIT
         ),
-    )(
-        pad, dense, cotangent, mask, kernel.reshape(TAPS * TAPS, channels),
-        gain.reshape(1, channels), w_in, w_in.T, w_out.T, embed, projection.T,
-    )
-
-
-def unpack_kernel(early, late, grad_projection, grad_kernel, grad_gain, grad_in, grad_out):
+    )(*fetched)
+
+
+def unpack_kernel(
+    early_hbm, late_hbm, state_hbm, embed_hbm,
+    grad_projection, grad_kernel, grad_gain, grad_in, grad_out, grad_state, grad_embed,
+    early, late, state, embed, load_sem, sems,
+):
+    loads = fetch(
+        (early_hbm, late_hbm, state_hbm, embed_hbm), (early, late, state, embed), load_sem
+    )
+    for load in loads:
+        load.wait()
+    moves = fetch((state, embed), (grad_state, grad_embed), sems)
     channels, hidden = grad_in.shape
+    features = grad_projection.shape[0]
     blocks = hidden // channels
-    grad_projection[...] = late[...].astype(jnp.float32)
+    grad_projection[...] = late[pl.ds(0, features)].astype(jnp.float32)
     for k in range(blocks):
         columns = slice(k * channels, (k + 1) * channels)
         grad_in[:, columns] = early[pl.ds(k * channels, channels)].astype(jnp.float32)
         grad_out[columns, :] = jnp.transpose(
             early[pl.ds((blocks + k) * channels, channels)].astype(jnp.float32)
         )
-    first = 2 * blocks * channels
-    small = early[pl.ds(first, early.shape[0] - first)].astype(jnp.float32)
+    small = late[pl.ds(features, late.shape[0] - features)].astype(jnp.float32)
     for a in range(TAPS):
         grad_kernel[a] = small[a * TAPS : (a + 1) * TAPS]
     grad_gain[...] = small[TAPS * TAPS : TAPS * TAPS + 1]
-
-
-def unpack(early, late, channels, hidden, features):
+    for move in moves:
+        move.wait()
+
+
+def unpack(early, late, state, embed, channels, hidden, features):
     shapes = (
         (features, channels), (TAPS, TAPS, channels), (1, channels),
-        (channels, hidden), (hidden, channels),
+        (channels, hidden), (hidden, channels), state.shape, embed.shape,
     )
     return pl.pallas_call(
         unpack_kernel,
         out_shape=tuple(jax.ShapeDtypeStruct(shape, jnp.float32) for shape in shapes),
-        in_specs=[pl.BlockSpec(memory_space=VMEM)] * 2,
-        out_specs=(pl.BlockSpec(memory_space=VMEM),) * 5,
-        compiler_params=pltpu.CompilerParams(vmem_limit_bytes=8 << 20),
-    )(early, late)
+        in_specs=[pl.BlockSpec(memory_space=pltpu.HBM)] * 4,
+        out_specs=(pl.BlockSpec(memory_space=VMEM),) * 5
+        + (pl.BlockSpec(memory_space=pltpu.HBM),) * 2,
+        scratch_shapes=[VMEM(array.shape, array.dtype) for array in (early, late, state, embed)]
+        + [pltpu.SemaphoreType.DMA((4,)), pltpu.SemaphoreType.DMA((2,))],
+        compiler_params=pltpu.CompilerParams(vmem_limit_bytes=LIMIT),
+    )(early, late, state, embed)
 
 
 def shards(
@@ -588,13 +651,13 @@
     sea_mask,
 ):
     channels, hidden = w_in.shape
-    pad, dense = forward(atm_embed, projection, margin_index, margin_weight, ocean_state)
-    grad_state, grad_embed, early, late = backward(
-        pad, dense, cotangent, sea_mask, dw_kernel, norm_gain, w_in, w_out, atm_embed, projection
-    )
-    grad_projection, grad_kernel, grad_gain, grad_in, grad_out = unpack(
-        early, late, channels, hidden, atm_embed.shape[1]
-    )
+    state, embed, early, late = whole(
+        jnp.transpose(margin_index, (1, 0, 2)), jnp.transpose(margin_weight, (1, 0, 2)),
+        atm_embed, projection, ocean_state, dw_kernel, cotangent, sea_mask, norm_gain,
+        w_in, w_out,
+    )
+    outs = unpack(early, late, state, embed, channels, hidden, atm_embed.shape[1])
+    grad_projection, grad_kernel, grad_gain, grad_in, grad_out, grad_state, grad_embed = outs
     return (
         grad_state, grad_embed, grad_projection, grad_kernel,
         grad_gain.reshape(channels), grad_in, grad_out,

time: 92.5 us -> 76 us (0.82)
  local copies, waits for them, and re-layouts: 12.3 us -> 0 us
  Pallas kernels: 79 us -> 75.2 us
    unnamed x21 -> x0, local copies, waits for them, and re-layouts: 11.5 us -> none
    pallas_call x2 -> x1, Pallas kernels: 78.1 us -> 71.6 us  [whole(): pl.pallas_call(functools.partial(whole_kernel, pow(STRIDE, -1, total), ea...]
    pallas_call x1, Pallas kernels: 0.88 us -> 3.6 us  [unpack(): pl.pallas_call(unpack_kernel, out_shape=tuple((jax.ShapeDtypeStruct(shape...]
where the time goes in v3:
time: 76 us; the launch traced here: 75.9 us
  Pallas kernels  75.2 us (99%)
    pallas_call x1, Pallas kernels, whole(): pl.pallas_call(functools.partial(whole_kernel, pow(STRIDE, -1, total), ea...  71.6 us
    pallas_call x1, Pallas kernels, unpack(): pl.pallas_call(unpack_kernel, out_shape=tuple((jax.ShapeDtypeStruct(shape...  3.6 us

profile of v3, /device:TPU:1, one launch (start us, length us, event | category | flops | bytes accessed | tf_op | source)
XLA Modules:
  0.0 75.9 jit_solution(1890306194797806339)
XLA Ops:
  0.6 71.6 %shard_map.162 = (f32[9,256,128]{2,1,0:T(8,128)}, f32[512,256]{1,0:T(8,128)}, bf16[1024,128]{1,0:T(8,128)(2,1)}, bf16[320,128]{1,0:T(8,128)(2,1)}) custom-call(s32[9,4,256]{2,1,0:T(4,128)} %bitcast.4, f32[9,4,256]{2,1,0:T(4,128)} %bitcast.5, bf16[512,256]{1,0:T(8,128)(2,1)} %embed_hbm.1, bf16[256,128]{1,0:T(8,128)(2,1)} %proj_hbm.1, ...), custom_call_target="tpu_custom_call" | custom-call | tf_op jit(solution)/shard_map/pallas_call | solution.py:542
  72.3 3.6 %shard_map.163 = (f32[256,128]{1,0:T(8,128)}, f32[7,7,128]{2,1,0:T(8,128)}, f32[1,128]{1,0:T(1,128)}, f32[128,512]{1,0:T(8,128)}, f32[512,128]{1,0:T(8,128)}, /*...) custom-call(bf16[1024,128]{1,0:T(8,128)(2,1)} %get-tuple-element.18.early_hbm, bf16[320,128]{1,0:T(8,128)(2,1)} %get-tuple-element.19.late_hbm, ...), custom_call_target="tpu_custom_call" | custom-call | tf_op jit(solution)/shard_map/pallas_call | solution.py:628

commit v4 on v3

--- a/solution.py
+++ b/solution.py
@@ -122,27 +122,52 @@
     return copies
 
 
-def greet_all(barrier):
+def greet_near(barrier):
     lat, lon, lats, lons = here()
-    columns = [lax.rem(lon + step, lons) for step in range(lons)]
-
-    def one(step, carry):
-        row = lax.rem(lat + step, lats)
-        for number, column in enumerate(columns):
-            def send(column=column):
-                pl.semaphore_signal(
-                    barrier, inc=1, device_id={"lat": row, "lon": column}, device_id_type=MESH
-                )
-
-            guarded(step > 0 if number == 0 else None, send)
-        return carry
-
-    lax.fori_loop(0, lats, one, 0)
+
+    def send(row, column):
+        pl.semaphore_signal(
+            barrier, inc=1, device_id={"lat": row, "lon": column}, device_id_type=MESH
+        )
+
+    left = lax.rem(lon + lons - 1, lons)
+    right = lax.rem(lon + 1, lons)
+
+    @pl.when(lat > 0)
+    def _():
+        send(lat - 1, left)
+        send(lat - 1, right)
+
+    @pl.when(lat < lats - 1)
+    def _():
+        send(lat + 1, left)
+        send(lat + 1, right)
+
+    for step in range(1, lons):
+        send(lat, lax.rem(lon + step, lons))
+    for step in range(1, lats):
+        send(lax.rem(lat + step, lats), lon)
+
+
+def wait_near(barrier):
+    lat, _, lats, lons = here()
+    ends = (lat == 0).astype(jnp.int32) + (lat == lats - 1).astype(jnp.int32)
+    pl.semaphore_wait(barrier, lats + lons + 2 - 2 * ends)
+
+
+def greet_row(round_sem):
+    lat, lon, lats, lons = here()
+    for step in range(1, lons):
+        pl.semaphore_signal(
+            round_sem, inc=1, device_id={"lat": lat, "lon": lax.rem(lon + step, lons)},
+            device_id_type=MESH,
+        )
 
 
 def forward_part(
-    barrier, embed_ref, index_ref, weight_ref, state_ref, proj_ref, loads, pad, dense, next_embed,
-    own, following, top_out, bottom_out, top_in, bottom_in,
+    barrier, round_sem, embed_ref, index_ref, weight_ref, state_ref, proj_ref, loads,
+    pad, dense, next_embed,
+    own, following, held, top_out, bottom_out, top_in, bottom_in,
     send_sem, recv_sem, window_send, window_recv, embed_send, embed_recv,
 ):
     lat, lon, lats, lons = here()
@@ -160,13 +185,18 @@
         factors = weight_ref[row]
         picks = [indices[q : q + 1, :] for q in range(margins)]
         weights = [factors[q : q + 1, :] for q in range(margins)]
+        merged = []
+        for q in range(margins):
+            sum_of = weights[q]
+            for p in range(q):
+                sum_of = sum_of + jnp.where(picks[p] == picks[q], weights[p], 0.0)
+            merged.append(sum_of)
         at = pl.ds(pl.multiple_of(row * width, 128), width)
         for start in range(0, slots, step):
             here_slots = base + start
-            total = None
-            for pick, weight in zip(picks, weights):
-                term = jnp.where(here_slots == pick, weight, 0.0)
-                total = term if total is None else total + term
+            total = jnp.zeros((step, width), jnp.float32)
+            for pick, weight in zip(picks, merged):
+                total = jnp.where(here_slots == pick, weight, total)
             dense[pl.ds(start, step), at] = total.astype(jnp.bfloat16)
         return carry
 
@@ -176,7 +206,8 @@
     proj_load.wait()
     projected = jnp.dot(embed_ref[...], proj_ref[...], preferred_element_type=jnp.float32)
     own[...] = jnp.transpose(projected).astype(jnp.bfloat16)
-    pl.semaphore_wait(barrier, lats * lons - 1)
+    wait_near(barrier)
+    greet_row(round_sem)
     window = pltpu.make_async_remote_copy(
         src_ref=own, dst_ref=following, send_sem=window_send, recv_sem=window_recv,
         device_id={"lat": lat - 1, "lon": lon}, device_id_type=MESH,
@@ -190,9 +221,8 @@
 
     def force_own(row, carry):
         at = pl.ds(pl.multiple_of(row * width, 128), width)
-        forcing = jnp.dot(own[...], dense[pl.ds(0, cells), at], preferred_element_type=jnp.float32)
-        pad[row + HALF, pl.ds(EDGE, width)] = (
-            state_ref[row].astype(jnp.float32) + jnp.transpose(forcing)
+        held[:, at] = jnp.dot(
+            own[...], dense[pl.ds(0, cells), at], preferred_element_type=jnp.float32
         )
         return carry
 
@@ -201,19 +231,23 @@
     @pl.when(lat == lats - 1)
     def _():
         next_embed[...] = jnp.zeros(next_embed.shape, jnp.bfloat16)
+        following[...] = jnp.zeros(following.shape, jnp.bfloat16)
 
     def force_next(row, carry):
         at = pl.ds(pl.multiple_of(row * width, 128), width)
         forcing = jnp.dot(
             following[...], dense[pl.ds(cells, cells), at], preferred_element_type=jnp.float32
         )
-        pad[row + HALF, pl.ds(EDGE, width)] += jnp.transpose(forcing)
+        pad[row + HALF, pl.ds(EDGE, width)] = state_ref[row].astype(
+            jnp.float32
+        ) + jnp.transpose(held[:, at] + forcing)
         return carry
 
     @pl.when(lat < lats - 1)
     def _():
         window.wait_recv()
-        lax.fori_loop(0, height, force_next, 0)
+
+    lax.fori_loop(0, height, force_next, 0)
 
     pl.when(lat > 0)(window.wait_send)
     rims = (pad, top_out, bottom_out, top_in, bottom_in, send_sem, recv_sem)
@@ -223,7 +257,7 @@
     return ahead
 
 
-def depthwise(pad, wide_kernel, out, height, width, flipped):
+def depthwise(pad, wide_kernel, out, height, columns, flipped):
     def block(column, carry):
         start = pl.multiple_of(column * EDGE, EDGE)
         near = pad.at[:, pl.ds(start, 3 * EDGE), :]
@@ -241,7 +275,7 @@
             out[r, pl.ds(start, EDGE), :] = sums[r]
         return carry
 
-    lax.fori_loop(0, width // EDGE, block, 0)
+    lax.fori_loop(columns[0], columns[1], block, 0)
 
 
 def kernel_grad(grad_pad, pad, small, height, width):
@@ -250,21 +284,21 @@
         offset = EDGE - HALF + b
 
         def block(column, sums):
-            start = pl.multiple_of(column * EDGE, EDGE)
-            near = pad.at[:, pl.ds(start, 3 * EDGE), :]
-            rows = [near[r, offset : offset + EDGE, :] for r in range(height + 2 * HALF)]
-            grads = [
-                grad_pad[r + HALF, pl.ds(pl.multiple_of(start + EDGE, EDGE), EDGE), :]
-                for r in range(height)
-            ]
+            start = pl.multiple_of(column * 2 * EDGE, EDGE)
+            near = pad.at[:, pl.ds(start, 4 * EDGE), :]
+            near_grad = grad_pad.at[:, pl.ds(start, 4 * EDGE), :]
             sums = list(sums)
-            for a in range(TAPS):
+            for extra in (0, EDGE):
+                at = offset + extra
+                rows = [near[r, at : at + EDGE, :] for r in range(height + 2 * HALF)]
                 for r in range(height):
-                    sums[a] = sums[a] + grads[r] * rows[r + a]
+                    grad = near_grad[r + HALF, EDGE + extra : 2 * EDGE + extra, :]
+                    for a in range(TAPS):
+                        sums[a] = sums[a] + grad * rows[r + a]
             return tuple(sums)
 
         zero = jnp.zeros((EDGE, channels), jnp.float32)
-        sums = lax.fori_loop(0, width // EDGE, block, (zero,) * TAPS)
+        sums = lax.fori_loop(0, width // (2 * EDGE), block, (zero,) * TAPS)
         for a in range(TAPS):
             small[pl.ds(a * TAPS + b, 1), :] = jnp.sum(sums[a], axis=0, keepdims=True)
 
@@ -359,13 +393,14 @@
     state_out, embed_out, early_out, late_out,
     index_ref, weight_ref, embed, proj, state_in, kernel_ref, cotangent, mask,
     gain_ref, w_in, w_out,
-    pad, dense, next_embed, own, following, x_top_out, x_bottom_out, x_top_in, x_bottom_in,
+    pad, dense, next_embed, own, following, held, x_top_out, x_bottom_out, x_top_in, x_bottom_in,
+    normed_rows, inv_rows, ln_row, g_y_row, g_ln_row,
     w_in_t, w_out_t, proj_t,
     wide_kernel, conv, grad_pad, state_low, g_window, grad_in, grad_out, small, gain_sum,
     back_out, back_in, g_embed, top_out, bottom_out, top_in, bottom_in,
     early_send, early_one, early_recv, late_send, late_one, late_recv,
     fetch_sem, x_send, x_recv, window_send, window_recv, ahead_send, ahead_recv,
-    halo_send, halo_recv, back_send, back_recv, early_sems, late_sems, move_sem,
+    halo_send, halo_recv, back_send, back_recv, early_sems, late_sems, move_sem, round_sem,
 ):
     lat, lon, lats, lons = here()
     height, width, channels = cotangent.shape
@@ -383,10 +418,11 @@
         fetch_sem,
     )
     barrier = pltpu.get_barrier_semaphore()
-    greet_all(barrier)
+    greet_near(barrier)
     ahead = forward_part(
-        barrier, embed, index_ref, weight_ref, state_in, proj, loads[:5], pad, dense, next_embed,
-        own, following, x_top_out, x_bottom_out, x_top_in, x_bottom_in,
+        barrier, round_sem, embed, index_ref, weight_ref, state_in, proj, loads[:5],
+        pad, dense, next_embed,
+        own, following, held, x_top_out, x_bottom_out, x_top_in, x_bottom_in,
         x_send, x_recv, window_send, window_recv, ahead_send, ahead_recv,
     )
     for load in loads[5:]:
@@ -396,7 +432,8 @@
         wide_kernel[tap] = jnp.broadcast_to(kernel_ref[a, b : b + 1, :], (EDGE, channels))
     for source, target in ((w_in, w_in_t), (w_out, w_out_t), (proj, proj_t)):
         target[...] = jnp.transpose(source[...].astype(jnp.float32)).astype(jnp.bfloat16)
-    depthwise(pad, wide_kernel, conv, height, width, False)
+    blocks_wide = width // EDGE
+    depthwise(pad, wide_kernel, conv, height, (0, blocks_wide), False)
     grad_in[...] = jnp.zeros(grad_in.shape, jnp.float32)
     grad_out[...] = jnp.zeros(grad_out.shape, jnp.float32)
     gain_sum[...] = jnp.zeros(gain_sum.shape, jnp.float32)
@@ -405,17 +442,23 @@
     c0 = 0.7978845608028654
     c1 = c0 * 0.044715
 
-    def row_step(row, carry):
+    def norm_of(row):
         field = conv[row]
         center = field - jnp.mean(field, axis=-1, keepdims=True)
         variance = jnp.mean(center * center, axis=-1, keepdims=True)
-        inv = lax.rsqrt(variance + EPSILON)
+        inv = jnp.broadcast_to(lax.rsqrt(variance + EPSILON), field.shape)
         normed = center * inv
-        ln = (normed * gain).astype(jnp.bfloat16)
         sea = jnp.transpose(
             jnp.broadcast_to(mask[pl.ds(row, 1), :].astype(jnp.float32), (channels, width))
         )
-        g_y = (cotangent[row].astype(jnp.float32) * sea).astype(jnp.bfloat16)
+        normed_rows[row] = normed
+        inv_rows[row] = inv
+        ln_row[...] = (normed * gain).astype(jnp.bfloat16)
+        g_y_row[...] = (cotangent[row].astype(jnp.float32) * sea).astype(jnp.bfloat16)
+
+    def mlp_of():
+        ln = ln_row[...]
+        g_y = g_y_row[...]
         g_ln = None
         for start in range(0, hidden, piece):
             part = slice(start, start + piece)
@@ -434,6 +477,11 @@
             )
             term = jnp.dot(g_pre, w_in_t[part, :], preferred_element_type=jnp.float32)
             g_ln = term if g_ln is None else g_ln + term
+        g_ln_row[...] = g_ln
+
+    def norm_back_of(row):
+        normed = normed_rows[row]
+        g_ln = g_ln_row[...]
         both = g_ln * normed
         gain_sum[...] += jnp.sum(both.reshape(width // EDGE, EDGE, channels), axis=0)
         g_n = g_ln * gain
@@ -441,11 +489,22 @@
             g_n
             - jnp.mean(g_n, axis=-1, keepdims=True)
             - normed * jnp.mean(both * gain, axis=-1, keepdims=True)
-        ) * inv
+        ) * inv_rows[row]
         grad_pad[row + HALF, pl.ds(EDGE, width)] = g_conv
+
+    def row_step(row, carry):
+        norm_back_of(row - 1)
+        mlp_of()
+        norm_of(row + 1)
         return carry
 
-    lax.fori_loop(0, height, row_step, 0)
+    norm_of(0)
+    mlp_of()
+    norm_of(1)
+    lax.fori_loop(1, height - 1, row_step, 0)
+    norm_back_of(height - 2)
+    mlp_of()
+    norm_back_of(height - 1)
     rims = (grad_pad, top_out, bottom_out, top_in, bottom_in, halo_send, halo_recv)
     halo_start(*rims)
 
@@ -457,6 +516,7 @@
             jnp.bfloat16
         )
     early = Summing(0, inverse, early_send, early_out, early_one, early_recv, early_sems)
+    pl.semaphore_wait(round_sem, lons - 1)
     early.scatter()
     small[...] = jnp.zeros(small.shape, jnp.float32)
     kernel_grad(grad_pad, pad, small, height, width)
@@ -464,7 +524,7 @@
     late_send[pl.ds(features, small.shape[0])] = small[...].astype(jnp.bfloat16)
     halo_finish(*rims)
 
-    depthwise(grad_pad, wide_kernel, conv, height, width, True)
+    depthwise(grad_pad, wide_kernel, conv, height, (0, blocks_wide), True)
 
     def state_step(row, carry):
         state = conv[row] + cotangent[row].astype(jnp.float32)
@@ -559,7 +619,13 @@
             VMEM((cells, features), low),
             VMEM((channels, cells), low),
             VMEM((channels, cells), low),
+            VMEM((channels, height * width), full),
             rim, rim, rim, rim,
+            VMEM((height, width, channels), full),
+            VMEM((height, width, channels), full),
+            VMEM((width, channels), low),
+            VMEM((width, channels), low),
+            VMEM((width, channels), full),
             VMEM((hidden, channels), low),
             VMEM((channels, hidden), low),
             VMEM((channels, features), low),
@@ -584,6 +650,7 @@
             VMEM(((total - 1) * ROWS, 128), low),
             dma((len(fetched),)), dma((8,)), dma((8,)), dma(()), dma(()), dma(()), dma(()),
             dma((8,)), dma((8,)), dma(()), dma(()), dma((4,)), dma((4,)), dma((2,)),
+            pltpu.SemaphoreType.REGULAR,
         ],
         compiler_params=pltpu.CompilerParams(
             collective_id=0, has_side_effects=True, vmem_limit_bytes=LIMIT
@@ -593,46 +660,68 @@
 
 def unpack_kernel(
     early_hbm, late_hbm, state_hbm, embed_hbm,
-    grad_projection, grad_kernel, grad_gain, grad_in, grad_out, grad_state, grad_embed,
-    early, late, state, embed, load_sem, sems,
+    projection_out, kernel_out, gain_out, in_out, out_out, state_out, embed_out,
+    early, late, state, embed, grad_projection, grad_kernel, grad_gain, grad_in, grad_out,
+    load_sem, sems,
 ):
     loads = fetch(
         (early_hbm, late_hbm, state_hbm, embed_hbm), (early, late, state, embed), load_sem
     )
-    for load in loads:
-        load.wait()
-    moves = fetch((state, embed), (grad_state, grad_embed), sems)
     channels, hidden = grad_in.shape
     features = grad_projection.shape[0]
     blocks = hidden // channels
-    grad_projection[...] = late[pl.ds(0, features)].astype(jnp.float32)
+    moves = [
+        pltpu.make_async_copy(source, target, sems.at[number])
+        for number, (source, target) in enumerate(
+            (
+                (state, state_out), (embed, embed_out), (grad_projection, projection_out),
+                (grad_kernel, kernel_out), (grad_gain, gain_out), (grad_in, in_out),
+                (grad_out, out_out),
+            )
+        )
+    ]
+    loads[0].wait()
     for k in range(blocks):
         columns = slice(k * channels, (k + 1) * channels)
         grad_in[:, columns] = early[pl.ds(k * channels, channels)].astype(jnp.float32)
-        grad_out[columns, :] = jnp.transpose(
-            early[pl.ds((blocks + k) * channels, channels)].astype(jnp.float32)
-        )
+    moves[5].start()
+    loads[1].wait()
+    grad_projection[...] = late[pl.ds(0, features)].astype(jnp.float32)
+    moves[2].start()
     small = late[pl.ds(features, late.shape[0] - features)].astype(jnp.float32)
     for a in range(TAPS):
         grad_kernel[a] = small[a * TAPS : (a + 1) * TAPS]
     grad_gain[...] = small[TAPS * TAPS : TAPS * TAPS + 1]
+    moves[3].start()
+    moves[4].start()
+    loads[2].wait()
+    moves[0].start()
+    loads[3].wait()
+    moves[1].start()
+    for k in range(blocks):
+        columns = slice(k * channels, (k + 1) * channels)
+        grad_out[columns, :] = jnp.transpose(
+            early[pl.ds((blocks + k) * channels, channels)].astype(jnp.float32)
+        )
+    moves[6].start()
     for move in moves:
         move.wait()
 
 
 def unpack(early, late, state, embed, channels, hidden, features):
-    shapes = (
+    grads = (
         (features, channels), (TAPS, TAPS, channels), (1, channels),
-        (channels, hidden), (hidden, channels), state.shape, embed.shape,
-    )
+        (channels, hidden), (hidden, channels),
+    )
+    shapes = grads + (state.shape, embed.shape)
     return pl.pallas_call(
         unpack_kernel,
         out_shape=tuple(jax.ShapeDtypeStruct(shape, jnp.float32) for shape in shapes),
         in_specs=[pl.BlockSpec(memory_space=pltpu.HBM)] * 4,
-        out_specs=(pl.BlockSpec(memory_space=VMEM),) * 5
-        + (pl.BlockSpec(memory_space=pltpu.HBM),) * 2,
+        out_specs=(pl.BlockSpec(memory_space=pltpu.HBM),) * 7,
         scratch_shapes=[VMEM(array.shape, array.dtype) for array in (early, late, state, embed)]
-        + [pltpu.SemaphoreType.DMA((4,)), pltpu.SemaphoreType.DMA((2,))],
+        + [VMEM(shape, jnp.float32) for shape in grads]
+        + [pltpu.SemaphoreType.DMA((4,)), pltpu.SemaphoreType.DMA((7,))],
         compiler_params=pltpu.CompilerParams(vmem_limit_bytes=LIMIT),
     )(early, late, state, embed)
 

time: 76 us -> 71.6 us (0.942)
  Pallas kernels: 75.2 us -> 70.8 us
    pallas_call x1, Pallas kernels: 71.6 us -> 68 us  [whole(): pl.pallas_call(functools.partial(whole_kernel, pow(STRIDE, -1, total), ea...]
    pallas_call x1, Pallas kernels: 3.6 us -> 2.76 us  [unpack(): pl.pallas_call(unpack_kernel, out_shape=tuple((jax.ShapeDtypeStruct(shape...]
where the time goes in v4:
time: 71.6 us; the launch traced here: 71.4 us
  Pallas kernels  70.8 us (99%)
    pallas_call x1, Pallas kernels, whole(): pl.pallas_call(functools.partial(whole_kernel, pow(STRIDE, -1, total), ea...  68 us
    pallas_call x1, Pallas kernels, unpack(): pl.pallas_call(unpack_kernel, out_shape=tuple((jax.ShapeDtypeStruct(shape...  2.76 us

profile of v4, /device:TPU:1, one launch (start us, length us, event | category | flops | bytes accessed | tf_op | source)
XLA Modules:
  0.0 71.4 jit_solution(11910111421410891062)
XLA Ops:
  0.6 68.0 %shard_map.162 = (f32[9,256,128]{2,1,0:T(8,128)}, f32[512,256]{1,0:T(8,128)}, bf16[1024,128]{1,0:T(8,128)(2,1)}, bf16[320,128]{1,0:T(8,128)(2,1)}) custom-call(s32[9,4,256]{2,1,0:T(4,128)} %bitcast.4, f32[9,4,256]{2,1,0:T(4,128)} %bitcast.5, bf16[512,256]{1,0:T(8,128)(2,1)} %embed_hbm.1, bf16[256,128]{1,0:T(8,128)(2,1)} %proj_hbm.1, ...), custom_call_target="tpu_custom_call" | custom-call | tf_op jit(solution)/shard_map/pallas_call | solution.py:602
  68.6 2.8 %shard_map.163 = (f32[256,128]{1,0:T(8,128)}, f32[7,7,128]{2,1,0:T(8,128)}, f32[1,128]{1,0:T(1,128)}, f32[128,512]{1,0:T(8,128)}, f32[512,128]{1,0:T(8,128)}, /*...) custom-call(bf16[1024,128]{1,0:T(8,128)(2,1)} %get-tuple-element.18.early_hbm, bf16[320,128]{1,0:T(8,128)(2,1)} %get-tuple-element.19.late_hbm, ...), custom_call_target="tpu_custom_call" | custom-call | tf_op jit(solution)/shard_map/pallas_call | solution.py:717

commit v5 on v4

--- a/solution.py
+++ b/solution.py
@@ -252,8 +252,8 @@
     pl.when(lat > 0)(window.wait_send)
     rims = (pad, top_out, bottom_out, top_in, bottom_in, send_sem, recv_sem)
     halo_start(*rims)
+    halo_finish(*rims)
     pl.when(lat > 0)(ahead.start)
-    halo_finish(*rims)
     return ahead
 
 
@@ -535,7 +535,6 @@
     lax.fori_loop(0, height, state_step, 0)
     state_move = pltpu.make_async_copy(conv, state_out, move_sem.at[0])
     state_move.start()
-    early.gather()
     chunk = 256
 
     def window_step(index, carry):
@@ -559,6 +558,7 @@
     ).astype(jnp.bfloat16)
     late = Summing(shift, inverse, late_send, late_out, late_one, late_recv, late_sems)
     late.scatter()
+    early.gather()
     back = pltpu.make_async_remote_copy(
         src_ref=back_out, dst_ref=back_in, send_sem=back_send, recv_sem=back_recv,
         device_id={"lat": lat + 1, "lon": lon}, device_id_type=MESH,

time: 71.6 us -> 70.2 us (0.980)
  Pallas kernels: 70.8 us -> 69.4 us
    pallas_call x1, Pallas kernels: 68 us -> 66.6 us  [whole(): pl.pallas_call(functools.partial(whole_kernel, pow(STRIDE, -1, total), ea...]
where the time goes in v5:
time: 70.2 us; the launch traced here: 70.1 us
  Pallas kernels  69.4 us (99%)
    pallas_call x1, Pallas kernels, whole(): pl.pallas_call(functools.partial(whole_kernel, pow(STRIDE, -1, total), ea...  66.6 us
    pallas_call x1, Pallas kernels, unpack(): pl.pallas_call(unpack_kernel, out_shape=tuple((jax.ShapeDtypeStruct(shape...  2.76 us

profile of v5, /device:TPU:1, one launch (start us, length us, event | category | flops | bytes accessed | tf_op | source)
XLA Modules:
  0.0 70.1 jit_solution(2096476843754458520)
XLA Ops:
  0.6 66.6 %shard_map.162 = (f32[9,256,128]{2,1,0:T(8,128)}, f32[512,256]{1,0:T(8,128)}, bf16[1024,128]{1,0:T(8,128)(2,1)}, bf16[320,128]{1,0:T(8,128)(2,1)}) custom-call(s32[9,4,256]{2,1,0:T(4,128)} %bitcast.4, f32[9,4,256]{2,1,0:T(4,128)} %bitcast.5, bf16[512,256]{1,0:T(8,128)(2,1)} %embed_hbm.1, bf16[256,128]{1,0:T(8,128)(2,1)} %proj_hbm.1, ...), custom_call_target="tpu_custom_call" | custom-call | tf_op jit(solution)/shard_map/pallas_call | solution.py:602
  67.3 2.8 %shard_map.163 = (f32[256,128]{1,0:T(8,128)}, f32[7,7,128]{2,1,0:T(8,128)}, f32[1,128]{1,0:T(1,128)}, f32[128,512]{1,0:T(8,128)}, f32[512,128]{1,0:T(8,128)}, /*...) custom-call(bf16[1024,128]{1,0:T(8,128)(2,1)} %get-tuple-element.18.early_hbm, bf16[320,128]{1,0:T(8,128)(2,1)} %get-tuple-element.19.late_hbm, ...), custom_call_target="tpu_custom_call" | custom-call | tf_op jit(solution)/shard_map/pallas_call | solution.py:717
